TPU v7x, 32 devices: a 4x2x2 block of a 4x4x8 slice. The times are simulated.
32 devices in a mesh: dp: 4 (over y, z), tp: 8 (over x, core).
Axes of the slice: x: 4, y: 2, z: 2, core: 2. Of those that a mesh axis runs over, the one named last changes fastest.
The devices are a block of a 4x4x8 slice.
Arguments:
- hidden_in: bfloat16 [4096, 2048], P(('dp', 'tp')), parts along dimension 0
- k_cache: bfloat16 [4096, 256, 256], P(('dp', 'tp')), parts along dimension 0
- v_cache: bfloat16 [4096, 256, 256], P(('dp', 'tp')), parts along dimension 0
- cache_len: int32 [4096], P(('dp', 'tp')), parts along dimension 0
- norm_attn: bfloat16 [2048], replicated
- norm_mlp: bfloat16 [2048], replicated
- w_q: bfloat16 [2048, 2048], replicated
- w_k: bfloat16 [2048, 256], replicated
- w_v: bfloat16 [2048, 256], replicated
- w_o: bfloat16 [2048, 2048], replicated
- w_gate: bfloat16 [2048, 16384], P(None, 'tp')
- w_up: bfloat16 [2048, 16384], P(None, 'tp')
- w_down: bfloat16 [16384, 2048], P('tp')
Outputs:
- output 1: bfloat16 [4096, 2048], P(('dp', 'tp')), parts along dimension 0
- output 2: bfloat16 [4096, 256], P(('dp', 'tp')), parts along dimension 0
- output 3: bfloat16 [4096, 256], P(('dp', 'tp')), parts along dimension 0
There are 4 independent parts. A program takes and returns all parts, laid end to end along the dimension named above; an argument that names none is the same for every part.
All inputs are finite; a program needn't handle non-finite values.
Results may differ from a plain program's by a relative error of at most 0.00561948.
Values are sent between devices in bfloat16 or wider.
A program may use at most 768 MiB of HBM per device.

v0:
```python
import jax
import jax.numpy as jnp
from jax import lax
from jax.sharding import PartitionSpec as P


def rms_scale(values, gain_vec):
    wide_vals = values.astype(jnp.float32)
    inv_rms = lax.rsqrt(jnp.mean(wide_vals * wide_vals, axis=-1, keepdims=True) + 1e-6)
    return (wide_vals * inv_rms * (1.0 + gain_vec.astype(jnp.float32))).astype(jnp.bfloat16)


def rope_tables(positions, head_dim):
    half_dim = head_dim // 2
    inv_freq = 10000.0 ** (-2.0 * jnp.arange(half_dim, dtype=jnp.float32) / head_dim)
    angles = positions.astype(jnp.float32)[:, None] * inv_freq[None, :]
    return jnp.cos(angles), jnp.sin(angles)


def rotary(values, cos_t, sin_t):
    half_dim = values.shape[-1] // 2
    first_half = values[..., :half_dim]
    second_half = values[..., half_dim:]
    return jnp.concatenate([first_half * cos_t - second_half * sin_t, second_half * cos_t + first_half * sin_t], axis=-1)


def attend(q_rot, k_new, v_new, k_cache, v_cache, cache_len):
    hist_score = jnp.einsum('bhd,btd->bht', q_rot, k_cache, preferred_element_type=jnp.float32)
    new_score = jnp.einsum('bhd,bd->bh', q_rot, k_new, preferred_element_type=jnp.float32)
    valid_mask = lax.broadcasted_iota(jnp.int32, (1, 1, k_cache.shape[1]), 2) < cache_len[:, None, None]
    hist_score = jnp.where(valid_mask, hist_score, -jnp.inf)
    peak_score = jnp.maximum(jnp.max(hist_score, axis=-1), new_score)
    hist_weight = jnp.exp(hist_score - peak_score[..., None])
    new_weight = jnp.exp(new_score - peak_score)
    weight_sum = jnp.sum(hist_weight, axis=-1) + new_weight
    hist_prob = (hist_weight / weight_sum[..., None]).astype(jnp.bfloat16)
    new_prob = (new_weight / weight_sum).astype(jnp.bfloat16)
    attn_out = jnp.einsum('bht,btd->bhd', hist_prob, v_cache, preferred_element_type=jnp.float32)
    attn_out = attn_out + new_prob.astype(jnp.float32)[..., None] * v_new.astype(jnp.float32)[:, None, :]
    return attn_out.astype(jnp.bfloat16)


def attention_block(hidden_in, k_cache, v_cache, cache_len, norm_attn, w_q, w_k, w_v, w_o):
    num_rows = hidden_in.shape[0]
    head_dim = w_k.shape[1]
    num_heads = w_q.shape[1] // head_dim
    normed = rms_scale(hidden_in, norm_attn)
    q_lin = jnp.dot(normed, w_q, preferred_element_type=jnp.float32).reshape(num_rows, num_heads, head_dim)
    k_lin = jnp.dot(normed, w_k, preferred_element_type=jnp.float32)
    v_new = jnp.dot(normed, w_v, preferred_element_type=jnp.float32).astype(jnp.bfloat16)
    cos_t, sin_t = rope_tables(cache_len, head_dim)
    q_rot = (rotary(q_lin, cos_t[:, None, :], sin_t[:, None, :]) * head_dim ** -0.5).astype(jnp.bfloat16)
    k_new = rotary(k_lin, cos_t, sin_t).astype(jnp.bfloat16)
    attn_out = attend(q_rot, k_new, v_new, k_cache, v_cache, cache_len)
    mixed = jnp.dot(attn_out.reshape(num_rows, num_heads * head_dim), w_o, preferred_element_type=jnp.float32)
    return hidden_in.astype(jnp.float32) + mixed, k_new, v_new


def solution(mesh):
    row_spec = P(('dp', 'tp'), None)
    cache_spec = P(('dp', 'tp'), None, None)
    full_vec = P(None)
    full_mat = P(None, None)

    def per_device(hidden_in, k_cache, v_cache, cache_len, norm_attn, norm_mlp, w_q, w_k, w_v, w_o, w_gate, w_up, w_down):
        x_mid, k_new, v_new = attention_block(hidden_in, k_cache, v_cache, cache_len, norm_attn, w_q, w_k, w_v, w_o)
        xn_mid = rms_scale(x_mid, norm_mlp)
        group_rows = lax.all_gather(xn_mid, 'tp', axis=0, tiled=True)
        gate_act = jnp.dot(group_rows, w_gate, preferred_element_type=jnp.float32)
        up_act = jnp.dot(group_rows, w_up, preferred_element_type=jnp.float32)
        hidden_act = (jax.nn.gelu(gate_act, approximate=True) * up_act).astype(jnp.bfloat16)
        part_sum = jnp.dot(hidden_act, w_down, preferred_element_type=jnp.float32)
        down_sum = lax.psum_scatter(part_sum, 'tp', scatter_dimension=0, tiled=True)
        return (x_mid + down_sum).astype(jnp.bfloat16), k_new, v_new

    return jax.shard_map(
        per_device,
        mesh=mesh,
        in_specs=(row_spec, cache_spec, cache_spec, P(('dp', 'tp')), full_vec, full_vec,
                  full_mat, full_mat, full_mat, full_mat, P(None, 'tp'), P(None, 'tp'), P('tp', None)),
        out_specs=(row_spec, row_spec, row_spec),
        check_vma=False,
    )
```

profile of v0, /device:TPU:81, one launch (start us, length us, event | category | flops | bytes accessed | tf_op | source)
XLA Modules:
  0.0 179.4 jit_solution(6017755065131428072)
XLA Ops:
  7.2 0.0 copy-start
  7.2 0.1 all-gather.2.cloned.1.call-start
  7.3 0.7 convert_element_type.50
  8.0 0.7 iota_compare_fusion
  8.8 1.2 fusion.15
  10.0 0.7 convert_add_fusion.1
  10.7 0.7 convert_add_fusion
  11.4 1.7 fusion.37
  13.1 0.0 copy-done
  13.1 2.0 %fusion.41 = (f32[128,256]{1,0:T(8,128)S(1)}, bf16[128,256]{1,0:T(8,128)(2,1)}) fusion(bf16[2048,256]{1,0:T(8,128)(2,1)S(1)} %copy-done, bf16[128,2048]{1,0:T(8,128)(2,1)} %param.13, f32[2048]{0:T(1024)S(1)} %convert_add_fusion.1, f32[128]{0:T(128)S(1)} %add_rsqrt_fusion.1), kind=kOutput, calls=%fused_computation.64 | convolution fusion | flops 135331840 | bytes 1778176 | tf_op jit(solution)/shard_map/dot_general | solution.py:50
  15.2 4.9 %fusion.39 = f32[128,2048]{1,0:T(8,128)S(1)} fusion(bf16[2048,2048]{1,0:T(8,128)(2,1)} %param.19, bf16[128,2048]{1,0:T(8,128)(2,1)} %param.13, f32[2048]{0:T(1024)S(1)} %convert_add_fusion.1, f32[128]{0:T(128)S(1)} %add_rsqrt_fusion.1), kind=kOutput, calls=%fused_computation.63 | convolution fusion | flops 1074790400 | bytes 9970176 | tf_op jit(solution)/shard_map/dot_general | solution.py:48
  20.0 0.3 copy.18
  20.4 0.3 subtract_convert_fusion
  20.7 0.1 multiply_subtract_fusion
  20.9 0.3 fusion.22
  21.1 10.3 %fusion.42 = (f32[128,8]{1,0:T(8,128)S(1)}, f32[128,8,256]{2,1,0:T(8,128)S(1)}) fusion(bf16[128,256,256]{2,1,0:T(8,128)(2,1)} %param.14, f32[128,8,128]{2,1,0:T(8,128)S(1)} %get-tuple-element.4, f32[128,8,128]{2,1,0:T(8,128)S(1)} %get-tuple-element.3, pred[128,256]{1,0:T(8,128)(4,1)S(1)} %iota_compare_fusion), kind=kOutput, calls=%fused_computation.65 | convolution fusion | flops 135527424 | bytes 18911232 | tf_op jit(solution)/shard_map/bhd,btd->bht/dot_general | solution.py:28
  31.4 0.0 slice-start
  31.5 0.4 fusion.19
  31.9 0.0 slice-start.1
  31.9 0.0 copy-start.2
  31.9 8.3 %fusion.14 = bf16[128,8,256]{2,1,0:T(8,128)(2,1)S(1)} fusion(bf16[128,256,256]{2,1,0:T(8,128)(2,1)} %param.15, f32[128,8,256]{2,1,0:T(8,128)S(1)} %get-tuple-element.14, f32[128,256]{1,0:T(8,128)S(1)} %get-tuple-element.11, f32[128,8]{1,0:T(8,128)S(1)} %get-tuple-element.6, f32[128,8]{1,0:T(8,128)S(1)} %get-tuple-element.5, f32[128,8]{1,0:T(8,128)S(1)} %max.3), kind=kOutput, calls=%fused_computation.20 | convolution fusion | flops 135790592 | bytes 18493440 | tf_op jit(solution)/shard_map/bht,btd->bhd/dot_general | solution.py:38
  40.2 0.1 copy.19
  40.3 0.0 slice-done
  40.4 0.0 slice-done.1
  40.4 0.0 copy-done.2
  40.4 1.4 multiply_reduce_fusion
  41.8 1.0 multiply_convert_fusion
  42.8 0.1 all-gather.2.cloned.1.call-update
  42.8 0.2 reduce-scatter.2.cloned.1.call-start
  43.1 33.2 %all-gather.2.cloned.1.call-done = bf16[1024,2048]{1,0:T(8,128)(2,1)} async-done(((bf16[128,2048]{1,0:T(8,128)(2,1)}), bf16[1024,2048]{1,0:T(8,128)(2,1)}) %all-gather.2.cloned.1.call-update) | async-done | bytes 4194320 | tf_op jit(solution)/shard_map/all_gather | solution.py:68
  76.2 14.5 %fusion.43 = f32[1024,2048]{1,0:T(8,128)} fusion(bf16[1024,2048]{1,0:T(8,128)(2,1)} %all-gather.2.cloned.1.call-done, bf16[2048,2048]{1,0:T(8,128)(2,1)} %param.23), kind=kOutput, calls=%fused_computation.66 | convolution fusion | flops 8589934592 | bytes 20971520 | tf_op jit(solution)/shard_map/dot_general | solution.py:69
  90.7 0.0 copy-start.1
  90.7 31.0 %fusion.9 = f32[1024,2048]{1,0:T(8,128)} fusion(bf16[2048,2048]{1,0:T(8,128)(2,1)} %param.25, f32[1024,2048]{1,0:T(8,128)} %fusion.43, bf16[1024,2048]{1,0:T(8,128)(2,1)} %all-gather.2.cloned.1.call-done, bf16[2048,2048]{1,0:T(8,128)(2,1)} %param.24), kind=kOutput, calls=%fused_computation.10 | convolution fusion | flops 17200840704 | bytes 37748736 | tf_op jit(solution)/shard_map/dot_general | solution.py:72
  121.8 0.1 reduce-scatter.2.cloned.1.call-update
  121.8 0.6 pad_maximum_fusion
  122.5 48.0 %reduce-scatter.2.cloned.1.call-done = f32[128,2048]{1,0:T(8,128)} async-done(((f32[1024,2048]{1,0:T(8,128)}), f32[128,2048]{1,0:T(8,128)}) %reduce-scatter.2.cloned.1.call-update) | async-done | bytes 1048592 | tf_op jit(solution)/shard_map/reduce_scatter | solution.py:73
  170.4 2.1 %add_convert_fusion = bf16[128,2048]{1,0:T(8,128)(2,1)} fusion(f32[128,2048]{1,0:T(8,128)S(1)} %get-tuple-element.16, f32[128,2048]{1,0:T(8,128)} %reduce-scatter.2.cloned.1.call-done), kind=kLoop, calls=%fused_computation.27 | loop fusion | flops 524288 | bytes 2621440 | tf_op jit(solution)/shard_map/convert_element_type | solution.py:74
  172.6 0.0 copy-done.1
  (7 shorter events, 0.1 us)
Async XLA Ops:
  7.2 6.0 %copy-start = (bf16[2048,256]{1,0:T(8,128)(2,1)S(1)}, bf16[2048,256]{1,0:T(8,128)(2,1)}, u32[]{:S(2)}) copy-start(bf16[2048,256]{1,0:T(8,128)(2,1)} %param.21) | copy-start | bytes 3145732
  7.2 69.0 %all-gather.2.cloned.1.call-start = ((), (), s32[]{:S(2)}) async-start(), calls=%async_computation.1 | async-start | bytes 4718592 | tf_op jit(solution)/shard_map/all_gather | solution.py:68
  31.4 8.9 %slice-start = ((s8[8388608]{0:T(1024)(128)(4,1)}), s8[4194304]{0:T(1024)(128)(4,1)S(1)}, s32[]{:S(2)}) async-start(s8[8388608]{0:T(1024)(128)(4,1)} %bitcast.20), calls=%async_computation.3 | async-start | bytes 8388608
  31.9 8.5 %slice-start.1 = ((s8[8388608]{0:T(1024)(128)(4,1)}), s8[4194304]{0:T(1024)(128)(4,1)S(1)}, s32[]{:S(2)}) async-start(s8[8388608]{0:T(1024)(128)(4,1)} %bitcast.20), calls=%async_computation.4 | async-start | bytes 8388608
  31.9 8.5 %copy-start.2 = (bf16[128,2048]{1,0:T(8,128)(2,1)S(1)}, bf16[128,2048]{1,0:T(8,128)(2,1)}, u32[]{:S(2)}) copy-start(bf16[128,2048]{1,0:T(8,128)(2,1)} %param.13) | copy-start | bytes 1572868
  42.8 127.6 %reduce-scatter.2.cloned.1.call-start = ((), (), s32[]{:S(2)}) async-start(), calls=%async_computation.2 | async-start | bytes 9437184 | tf_op jit(solution)/shard_map/reduce_scatter | solution.py:73
  90.7 81.8 %copy-start.1 = (bf16[2048,256]{1,0:T(8,128)(2,1)S(1)}, bf16[2048,256]{1,0:T(8,128)(2,1)}, u32[]{:S(2)}) copy-start(bf16[2048,256]{1,0:T(8,128)(2,1)} %param.21) | copy-start | bytes 3145732
Sparse Core Ops, SparseCore 0:
  42.9 33.2 all-gather.1
  121.9 48.4 reduce-scatter.1
where the time goes:
time: 180 us; the launch traced here: 179 us
  waiting for transfers between devices  81.3 us (45%)
  matrix products  74.4 us (41%)
  between operations  14.2 us (8%)
  other arithmetic  8.7 us (5%)
    reduce_scatter x1, waiting for transfers between devices, per_device(): down_sum = lax.psum_scatter(part_sum, 'tp', scatter_dimension=0, tiled=True)  48 us
    all_gather x1, waiting for transfers between devices, per_device(): group_rows = lax.all_gather(xn_mid, 'tp', axis=0, tiled=True)  33.2 us
    dot_general x1, matrix products, per_device(): part_sum = jnp.dot(hidden_act, w_down, preferred_element_type=jnp.float32)  31 us
    dot_general x1, matrix products, per_device(): gate_act = jnp.dot(group_rows, w_gate, preferred_element_type=jnp.float32)  14.5 us
    dot_general x1, matrix products, attend(): jnp.einsum('bhd,btd->bht', q_rot, k_cache, preferred_element_type=jnp.flo...  10.3 us
    dot_general x1, matrix products, attend(): jnp.einsum('bht,btd->bhd', hist_prob, v_cache, preferred_element_type=jnp...  8.32 us
    dot_general x1, matrix products, attention_block(): jnp.dot(normed, w_q, preferred_element_type=jnp.float32)  4.87 us
  transfers between devices with their start and end apart: 2, of which 2 were waited for; matrix products, arithmetic and copies ran while one was open for 0% of the time, Pallas kernels for 0%

commit v1 on v0

--- a/solution.py
+++ b/solution.py
@@ -1,7 +1,13 @@
+import functools
+
 import jax
 import jax.numpy as jnp
 from jax import lax
+from jax.experimental import pallas as pl
+from jax.experimental.pallas import tpu as pltpu
 from jax.sharding import PartitionSpec as P
+
+MESH = pl.DeviceIdType.MESH
 
 
 def rms_scale(values, gain_vec):
@@ -56,6 +62,194 @@
     return hidden_in.astype(jnp.float32) + mixed, k_new, v_new
 
 
+def mlp_kernel(half, tile, depth_tile, xn_ref, x_ref, wg_hbm, wu_hbm, wd_hbm, out_ref,
+               wg, wu, wd, xb, hid, own, snd, prt, ring,
+               w_sem, ag_send, ag_recv, d_send, d_recv, r_send, r_recv):
+    chips = lax.axis_size('tp') // 2
+    me = lax.axis_index('tp')
+    core = lax.rem(me, 2)
+    chip = me // 2
+    partner = me + 1 - 2 * core
+    ahead = 2 * lax.rem(chip + 1, chips) + core
+    behind = 2 * lax.rem(chip + chips - 1, chips) + core
+    rows = 2 * half
+    n_up = wg.shape[0]
+    n_down = wd.shape[0]
+
+    def to(src, dst, send, recv, dev):
+        return pltpu.make_async_remote_copy(src_ref=src, dst_ref=dst, send_sem=send, recv_sem=recv,
+                                            device_id={'tp': dev}, device_id_type=MESH)
+
+    barrier = pltpu.get_barrier_semaphore()
+    for dev in (partner, ahead, behind):
+        pl.semaphore_signal(barrier, inc=1, device_id={'tp': dev}, device_id_type=MESH)
+
+    def up_load(i, n):
+        src, dst = ((wg_hbm, wg), (wu_hbm, wu))[i]
+        return pltpu.make_async_copy(src.at[:, pl.ds(n * tile, tile)], dst.at[n], w_sem.at[i, n])
+
+    def down_load(n):
+        return pltpu.make_async_copy(wd_hbm.at[:, pl.ds(n * depth_tile, depth_tile)], wd.at[n], w_sem.at[2, n])
+
+    for n in range(n_up):
+        up_load(0, n).start()
+        up_load(1, n).start()
+    for n in range(n_down):
+        down_load(n).start()
+
+    lo, hi = pl.ds(0, half), pl.ds(half, half)
+    mine, theirs = pl.ds(0, rows), pl.ds(rows, rows)
+    pl.semaphore_wait(barrier, 3)
+
+    gather = [
+        to(xn_ref, xb.at[0, theirs], ag_send.at[0], ag_recv.at[0], partner),
+        to(xn_ref.at[lo], xb.at[1, hi], ag_send.at[1], ag_recv.at[1], ahead),
+        to(xn_ref.at[hi], xb.at[1, lo], ag_send.at[2], ag_recv.at[2], behind),
+        to(xn_ref.at[hi], xb.at[2, hi], ag_send.at[3], ag_recv.at[3], ahead),
+        to(xn_ref.at[lo], xb.at[2, lo], ag_send.at[4], ag_recv.at[4], behind),
+        to(xb.at[1, hi], xb.at[3, lo], ag_send.at[5], ag_recv.at[5], ahead),
+        to(xb.at[1, lo], xb.at[3, hi], ag_send.at[6], ag_recv.at[6], behind),
+        to(xb.at[1, mine], xb.at[1, theirs], ag_send.at[7], ag_recv.at[7], partner),
+        to(xb.at[2, mine], xb.at[2, theirs], ag_send.at[8], ag_recv.at[8], partner),
+        to(xb.at[3, mine], xb.at[3, theirs], ag_send.at[9], ag_recv.at[9], partner),
+    ]
+    for copy in gather[:5]:
+        copy.start()
+    xb[0, 0:rows, :] = xn_ref[...]
+
+    def up(b):
+        def body(n, carry):
+            if b == 0:
+                up_load(0, n).wait()
+                up_load(1, n).wait()
+            gate = jnp.dot(xb[b], wg[n], preferred_element_type=jnp.float32)
+            lin = jnp.dot(xb[b], wu[n], preferred_element_type=jnp.float32)
+            act = jax.nn.gelu(gate, approximate=True) * lin
+            hid[:, pl.ds(pl.multiple_of(n * tile, tile), tile)] = act.astype(jnp.bfloat16)
+            return carry
+        lax.fori_loop(0, n_up, body, 0)
+
+    def exchange(b, n):
+        return to(snd.at[b, n], prt.at[b, n], d_send.at[b, n], d_recv.at[b, n], partner)
+
+    def hops(step, b, n):
+        return (to(own.at[b, n, lo], ring.at[step, n, lo], r_send.at[step, 0, n], r_recv.at[step, 0, n], ahead),
+                to(own.at[b, n, hi], ring.at[step, n, hi], r_send.at[step, 1, n], r_recv.at[step, 1, n], behind))
+
+    def merge(b, n, step):
+        exchange(b, n).wait_recv()
+        own[b, n] = own[b, n] + prt[b, n]
+        if step is not None:
+            for copy in hops(step, b, n):
+                copy.start()
+
+    def down(b, step):
+        def body(n, carry):
+            if b == 0:
+                down_load(n).wait()
+            part = jnp.dot(hid[...], wd[n], preferred_element_type=jnp.float32)
+            own[b, n] = part[0:rows]
+            snd[b, n] = part[rows:2 * rows]
+            exchange(b, n).start()
+            @pl.when(n > 0)
+            def _():
+                merge(b, n - 1, step)
+            return carry
+        lax.fori_loop(0, n_down, body, 0)
+        merge(b, n_down - 1, step)
+
+    gather[0].wait_recv()
+    up(0)
+    down(0, None)
+    gather[1].wait_recv()
+    gather[2].wait_recv()
+    gather[7].start()
+    gather[5].start()
+    gather[6].start()
+    gather[7].wait_recv()
+    up(1)
+    gather[3].wait_recv()
+    gather[4].wait_recv()
+    gather[8].start()
+    down(1, 0)
+    gather[8].wait_recv()
+    up(2)
+    gather[5].wait_recv()
+    gather[6].wait_recv()
+    gather[9].start()
+    down(2, None)
+    gather[9].wait_recv()
+    up(3)
+    down(3, 1)
+
+    def relay(n, carry):
+        for copy in hops(1, 3, n):
+            copy.wait_recv()
+        own[2, n] = own[2, n] + ring[1, n]
+        for copy in hops(2, 2, n):
+            copy.start()
+        for copy in hops(0, 1, n):
+            copy.wait_recv()
+        own[0, n, lo] = own[0, n, lo] + ring[0, n, hi]
+        own[0, n, hi] = own[0, n, hi] + ring[0, n, lo]
+        return carry
+    lax.fori_loop(0, n_down, relay, 0)
+
+    def finish(n, carry):
+        for copy in hops(2, 2, n):
+            copy.wait_recv()
+        cols = pl.ds(pl.multiple_of(n * depth_tile, depth_tile), depth_tile)
+        out_ref[:, cols] = (x_ref[:, cols] + (own[0, n] + ring[2, n])).astype(jnp.bfloat16)
+        return carry
+    lax.fori_loop(0, n_down, finish, 0)
+
+    for copy in gather:
+        copy.wait_send()
+    def drain(n, carry):
+        for b in range(4):
+            exchange(b, n).wait_send()
+        for step, b in ((0, 1), (1, 3), (2, 2)):
+            for copy in hops(step, b, n):
+                copy.wait_send()
+        return carry
+    lax.fori_loop(0, n_down, drain, 0)
+
+
+def mlp(xn, x_mid, w_gate, w_up, w_down):
+    rows, width = xn.shape
+    units = w_gate.shape[1]
+    tile = 512
+    depth_tile = 512
+    n_up, n_down = units // tile, width // depth_tile
+    sems = pltpu.SemaphoreType.DMA
+    vmem = pl.BlockSpec(memory_space=pltpu.VMEM)
+    hbm = pl.BlockSpec(memory_space=pl.ANY)
+    return pl.pallas_call(
+        functools.partial(mlp_kernel, rows // 2, tile, depth_tile),
+        out_shape=jax.ShapeDtypeStruct((rows, width), jnp.bfloat16),
+        in_specs=[vmem, vmem, hbm, hbm, hbm],
+        out_specs=vmem,
+        scratch_shapes=[
+            pltpu.VMEM((n_up, width, tile), jnp.bfloat16),
+            pltpu.VMEM((n_up, width, tile), jnp.bfloat16),
+            pltpu.VMEM((n_down, units, depth_tile), jnp.bfloat16),
+            pltpu.VMEM((4, 2 * rows, width), jnp.bfloat16),
+            pltpu.VMEM((2 * rows, units), jnp.bfloat16),
+            pltpu.VMEM((4, n_down, rows, depth_tile), jnp.float32),
+            pltpu.VMEM((4, n_down, rows, depth_tile), jnp.float32),
+            pltpu.VMEM((4, n_down, rows, depth_tile), jnp.float32),
+            pltpu.VMEM((3, n_down, rows, depth_tile), jnp.float32),
+            sems((3, max(n_up, n_down))),
+            sems((10,)), sems((10,)),
+            sems((4, n_down)), sems((4, n_down)),
+            sems((3, 2, n_down)), sems((3, 2, n_down)),
+        ],
+        compiler_params=pltpu.CompilerParams(collective_id=0, has_side_effects=True, vmem_limit_bytes=60 * 1024 * 1024),
+        cost_estimate=pl.CostEstimate(flops=2 * 8 * rows * width * units * 3, bytes_accessed=6 * width * units, transcendentals=0),
+        name='mlp',
+    )(xn, x_mid, w_gate, w_up, w_down)
+
+
 def solution(mesh):
     row_spec = P(('dp', 'tp'), None)
     cache_spec = P(('dp', 'tp'), None, None)
@@ -65,13 +259,7 @@
     def per_device(hidden_in, k_cache, v_cache, cache_len, norm_attn, norm_mlp, w_q, w_k, w_v, w_o, w_gate, w_up, w_down):
         x_mid, k_new, v_new = attention_block(hidden_in, k_cache, v_cache, cache_len, norm_attn, w_q, w_k, w_v, w_o)
         xn_mid = rms_scale(x_mid, norm_mlp)
-        group_rows = lax.all_gather(xn_mid, 'tp', axis=0, tiled=True)
-        gate_act = jnp.dot(group_rows, w_gate, preferred_element_type=jnp.float32)
-        up_act = jnp.dot(group_rows, w_up, preferred_element_type=jnp.float32)
-        hidden_act = (jax.nn.gelu(gate_act, approximate=True) * up_act).astype(jnp.bfloat16)
-        part_sum = jnp.dot(hidden_act, w_down, preferred_element_type=jnp.float32)
-        down_sum = lax.psum_scatter(part_sum, 'tp', scatter_dimension=0, tiled=True)
-        return (x_mid + down_sum).astype(jnp.bfloat16), k_new, v_new
+        return mlp(xn_mid, x_mid, w_gate, w_up, w_down), k_new, v_new
 
     return jax.shard_map(
         per_device,

time: 180 us -> 109 us (0.61)
  waiting for transfers between devices: 81.3 us -> 0 us
  Pallas kernels: 0 us -> 71.4 us
  matrix products: 74.4 us -> 28.2 us
  between operations: 14.2 us -> 0.84 us
  other arithmetic: 8.7 us -> 5.41 us
  local copies, waits for them, and re-layouts: 0.5 us -> 2.88 us
    pallas_call x0 -> x1, Pallas kernels: none -> 71.4 us  [mlp(): pl.pallas_call(functools.partial(mlp_kernel, rows // 2, tile, depth_tile)...]
    reduce_scatter x1 -> x0, waiting for transfers between devices: 48 us -> none  [per_device(): down_sum = lax.psum_scatter(part_sum, 'tp', scatter_dimension=0, tiled=True)]
    dot_general x2 -> x0, matrix products: 45.5 us -> none  [the longest x1 31 us: per_device(): part_sum = jnp.dot(hidden_act, w_down, preferred_element_type=jnp.float32)]
    all_gather x1 -> x0, waiting for transfers between devices: 33.2 us -> none  [per_device(): group_rows = lax.all_gather(xn_mid, 'tp', axis=0, tiled=True)]
    unnamed x12 -> x21, local copies, waits for them, and re-layouts: 0.5 us -> 2.88 us
    convert_element_type x1 -> x0, other arithmetic: 2.12 us -> none  [per_device(): return ((x_mid + down_sum).astype(jnp.bfloat16), k_new, v_new)]
  transfers between devices with their start and end apart: 2 -> 0, of which waited for: 2 -> 0; matrix products, arithmetic and copies ran while one was open for 0% -> 0% of each run, Pallas kernels for 0% -> 0%
where the time goes in v1:
time: 109 us
  Pallas kernels  71.4 us (66%)
  matrix products  28.2 us (26%)
  other arithmetic  5.41 us (5%)
  local copies, waits for them, and re-layouts  2.88 us (3%)
    pallas_call x1, Pallas kernels, mlp(): pl.pallas_call(functools.partial(mlp_kernel, rows // 2, tile, depth_tile)...  71.4 us
    dot_general x1, matrix products, attend(): jnp.einsum('bhd,btd->bht', q_rot, k_cache, preferred_element_type=jnp.flo...  10.5 us
    dot_general x1, matrix products, attend(): jnp.einsum('bht,btd->bhd', hist_prob, v_cache, preferred_element_type=jnp...  8.39 us
    dot_general x1, matrix products, attention_block(): jnp.dot(normed, w_q, preferred_element_type=jnp.float32)  4.87 us
    unnamed x21, local copies, waits for them, and re-layouts  2.88 us

profile of v1, /device:TPU:81, one launch (start us, length us, event | category | flops | bytes accessed | tf_op | source)
XLA Modules:
  0.0 108.7 jit_solution(945212141849511646)
XLA Ops:
  0.6 0.0 copy-start
  0.6 0.8 convert_add_fusion.1
  1.4 1.2 %fusion.1 = f32[128]{0:T(128)S(1)} fusion(bf16[128,2048]{1,0:T(8,128)(2,1)} %param.13), kind=kLoop, calls=%fused_computation.7 | loop fusion | flops 786304 | bytes 524800 | tf_op jit(solution)/shard_map/reduce_sum | solution.py:15
  2.7 1.7 %fusion.19 = f32[128,256]{1,0:T(8,128)S(1)} fusion(bf16[2048,256]{1,0:T(8,128)(2,1)} %param.20, bf16[128,2048]{1,0:T(8,128)(2,1)} %param.13, f32[2048]{0:T(1024)S(1)} %convert_add_fusion.1, f32[128]{0:T(128)S(1)} %add_rsqrt_fusion.1), kind=kOutput, calls=%fused_computation.42 | convolution fusion | flops 135266304 | bytes 1712640 | tf_op jit(solution)/shard_map/dot_general | solution.py:55
  4.4 0.7 convert_element_type.44
  5.1 0.3 subtract_convert_fusion
  5.4 0.0 copy-start.6
  5.4 4.9 %fusion.21 = f32[128,2048]{1,0:T(8,128)S(1)} fusion(bf16[2048,2048]{1,0:T(8,128)(2,1)} %param.19, bf16[128,2048]{1,0:T(8,128)(2,1)} %param.13, f32[2048]{0:T(1024)S(1)} %convert_add_fusion.1, f32[128]{0:T(128)S(1)} %add_rsqrt_fusion.1), kind=kOutput, calls=%fused_computation.43 | convolution fusion | flops 1074790400 | bytes 9970176 | tf_op jit(solution)/shard_map/dot_general | solution.py:54
  10.3 0.3 copy.18
  10.7 0.1 multiply_subtract_fusion
  10.8 0.0 copy-start.4
  10.8 0.3 fusion.8
  11.1 0.5 copy-done.4
  11.6 0.0 copy-done.6
  11.6 0.1 iota_compare_fusion
  11.7 0.0 copy-start.2
  11.7 10.5 %fusion.24 = (f32[128,8]{1,0:T(8,128)S(1)}, f32[128,8,256]{2,1,0:T(8,128)S(1)}) fusion(bf16[128,256,256]{2,1,0:T(8,128)(2,1)} %param.14, f32[128,8,128]{2,1,0:T(8,128)} %copy-done.4, f32[128,8,128]{2,1,0:T(8,128)S(1)} %get-tuple-element.3, pred[128,256]{1,0:T(8,128)(4,1)S(1)} %iota_compare_fusion), kind=kOutput, calls=%fused_computation.45 | convolution fusion | flops 135527424 | bytes 18911232 | tf_op jit(solution)/shard_map/bhd,btd->bht/dot_general | solution.py:34
  22.2 0.4 fusion.5
  22.6 0.0 copy-done
  22.6 0.0 copy-done.2
  22.7 0.0 slice-start
  22.7 1.0 fusion.23
  23.7 0.0 slice-start.1
  23.7 8.4 %fusion = bf16[128,8,256]{2,1,0:T(8,128)(2,1)S(1)} fusion(bf16[128,256,256]{2,1,0:T(8,128)(2,1)} %param.15, f32[128,8,256]{2,1,0:T(8,128)S(1)} %get-tuple-element.14, f32[128,256]{1,0:T(8,128)S(1)} %get-tuple-element.11, f32[128,8]{1,0:T(8,128)S(1)} %get-tuple-element.6, f32[128,8]{1,0:T(8,128)S(1)} %get-tuple-element.5, f32[128,8]{1,0:T(8,128)S(1)} %max.3), kind=kOutput, calls=%fused_computation.5 | convolution fusion | flops 135790592 | bytes 18493440 | tf_op jit(solution)/shard_map/bht,btd->bhd/dot_general | solution.py:44
  32.1 0.0 copy-start.5
  32.1 0.1 copy.19
  32.2 0.0 slice-done
  32.2 0.0 slice-done.1
  32.2 1.4 %multiply_reduce_fusion = (f32[128]{0:T(128)S(1)}, f32[128,2048]{1,0:T(8,128)S(1)}) fusion(bf16[128,2048]{1,0:T(8,128)(2,1)S(1)} %bitcast.20, bf16[2048,2048]{1,0:T(8,128)(2,1)S(1)} %bitcast.16, bf16[128,2048]{1,0:T(8,128)(2,1)S(1)} %copy-done.2), kind=kOutput, calls=%fused_computation.13 | convolution fusion | flops 1074790272 | bytes 10486272 | tf_op jit(solution)/shard_map/dot_general | solution.py:61
  33.6 0.0 copy-start.3
  33.6 0.0 copy-done.5
  33.7 1.1 %multiply_convert_fusion.xn_ref = bf16[128,2048]{1,0:T(8,128)(2,1)} fusion(f32[128,2048]{1,0:T(8,128)S(1)} %get-tuple-element.16.x_ref, f32[2048]{0:T(1024)S(1)} %convert_add_fusion, f32[128]{0:T(128)S(1)} %add_rsqrt_fusion), kind=kLoop, calls=%fused_computation.12 | loop fusion | flops 786432 | bytes 1581568 | tf_op jit(solution)/shard_map/convert_element_type | solution.py:16
  34.8 0.0 copy-done.3
  34.8 0.0 copy-start.1
  34.8 71.4 %mlp.1 = bf16[128,2048]{1,0:T(8,128)(2,1)} custom-call(bf16[128,2048]{1,0:T(8,128)(2,1)} %multiply_convert_fusion.xn_ref, f32[128,2048]{1,0:T(8,128)} %copy-done.3, bf16[2048,2048]{1,0:T(8,128)(2,1)} %wg_hbm.1, bf16[2048,2048]{1,0:T(8,128)(2,1)} %wu_hbm.1, bf16[2048,2048]{1,0:T(8,128)(2,1)} %wd_hbm.1), custom_call_target="tpu_custom_call" | custom-call | flops 25769803776 | bytes 25165824 | tf_op jit(solution)/shard_map/mlp/pallas_call | solution.py:227
  106.2 0.6 pad_maximum_fusion
  106.8 1.9 %copy.23 = bf16[128,2048]{1,0:T(8,128)(2,1)} copy(bf16[128,2048]{1,0:T(8,128)(2,1)} %mlp.1) | data formatting | bytes 1048576
  108.7 0.0 copy-done.1
  (8 shorter events, 0.1 us)
Async XLA Ops:
  0.6 22.0 %copy-start = (bf16[2048,256]{1,0:T(8,128)(2,1)S(1)}, bf16[2048,256]{1,0:T(8,128)(2,1)}, u32[]{:S(2)}) copy-start(bf16[2048,256]{1,0:T(8,128)(2,1)} %param.21) | copy-start | bytes 3145732
  5.4 6.2 %copy-start.6 = (s32[128]{0:T(128)S(1)}, s32[128]{0:T(128)}, u32[]{:S(2)}) copy-start(s32[128]{0:T(128)} %param.16) | copy-start | bytes 1540
  10.8 0.8 copy-start.4
  11.7 11.0 %copy-start.2 = (bf16[128,2048]{1,0:T(8,128)(2,1)S(1)}, bf16[128,2048]{1,0:T(8,128)(2,1)}, u32[]{:S(2)}) copy-start(bf16[128,2048]{1,0:T(8,128)(2,1)} %param.13) | copy-start | bytes 1572868
  22.7 9.5 %slice-start = ((s8[8388608]{0:T(1024)(128)(4,1)}), s8[4194304]{0:T(1024)(128)(4,1)S(1)}, s32[]{:S(2)}) async-start(s8[8388608]{0:T(1024)(128)(4,1)} %bitcast.15), calls=%async_computation | async-start | bytes 8388608
  23.7 8.5 %slice-start.1 = ((s8[8388608]{0:T(1024)(128)(4,1)}), s8[4194304]{0:T(1024)(128)(4,1)S(1)}, s32[]{:S(2)}) async-start(s8[8388608]{0:T(1024)(128)(4,1)} %bitcast.15), calls=%async_computation.1 | async-start | bytes 8388608
  32.1 1.6 %copy-start.5 = (bf16[2048]{0:T(1024)(128)(2,1)S(1)}, bf16[2048]{0:T(1024)(128)(2,1)}, u32[]{:S(2)}) copy-start(bf16[2048]{0:T(1024)(128)(2,1)} %param.18) | copy-start | bytes 12292
  33.6 1.1 %copy-start.3 = (f32[128,2048]{1,0:T(8,128)}, f32[128,2048]{1,0:T(8,128)S(1)}, u32[]{:S(2)}) copy-start(f32[128,2048]{1,0:T(8,128)S(1)} %get-tuple-element.16.x_ref) | copy-start | bytes 3145732
  34.8 74.0 %copy-start.1 = (bf16[2048,256]{1,0:T(8,128)(2,1)S(1)}, bf16[2048,256]{1,0:T(8,128)(2,1)}, u32[]{:S(2)}) copy-start(bf16[2048,256]{1,0:T(8,128)(2,1)} %param.21) | copy-start | bytes 3145732

commit v2 on v1

--- a/solution.py
+++ b/solution.py
@@ -10,56 +10,172 @@
 MESH = pl.DeviceIdType.MESH
 
 
-def rms_scale(values, gain_vec):
-    wide_vals = values.astype(jnp.float32)
-    inv_rms = lax.rsqrt(jnp.mean(wide_vals * wide_vals, axis=-1, keepdims=True) + 1e-6)
-    return (wide_vals * inv_rms * (1.0 + gain_vec.astype(jnp.float32))).astype(jnp.bfloat16)
-
-
-def rope_tables(positions, head_dim):
-    half_dim = head_dim // 2
-    inv_freq = 10000.0 ** (-2.0 * jnp.arange(half_dim, dtype=jnp.float32) / head_dim)
-    angles = positions.astype(jnp.float32)[:, None] * inv_freq[None, :]
-    return jnp.cos(angles), jnp.sin(angles)
-
-
-def rotary(values, cos_t, sin_t):
-    half_dim = values.shape[-1] // 2
-    first_half = values[..., :half_dim]
-    second_half = values[..., half_dim:]
-    return jnp.concatenate([first_half * cos_t - second_half * sin_t, second_half * cos_t + first_half * sin_t], axis=-1)
-
-
-def attend(q_rot, k_new, v_new, k_cache, v_cache, cache_len):
-    hist_score = jnp.einsum('bhd,btd->bht', q_rot, k_cache, preferred_element_type=jnp.float32)
-    new_score = jnp.einsum('bhd,bd->bh', q_rot, k_new, preferred_element_type=jnp.float32)
-    valid_mask = lax.broadcasted_iota(jnp.int32, (1, 1, k_cache.shape[1]), 2) < cache_len[:, None, None]
-    hist_score = jnp.where(valid_mask, hist_score, -jnp.inf)
-    peak_score = jnp.maximum(jnp.max(hist_score, axis=-1), new_score)
-    hist_weight = jnp.exp(hist_score - peak_score[..., None])
-    new_weight = jnp.exp(new_score - peak_score)
-    weight_sum = jnp.sum(hist_weight, axis=-1) + new_weight
-    hist_prob = (hist_weight / weight_sum[..., None]).astype(jnp.bfloat16)
-    new_prob = (new_weight / weight_sum).astype(jnp.bfloat16)
-    attn_out = jnp.einsum('bht,btd->bhd', hist_prob, v_cache, preferred_element_type=jnp.float32)
-    attn_out = attn_out + new_prob.astype(jnp.float32)[..., None] * v_new.astype(jnp.float32)[:, None, :]
-    return attn_out.astype(jnp.bfloat16)
-
-
-def attention_block(hidden_in, k_cache, v_cache, cache_len, norm_attn, w_q, w_k, w_v, w_o):
-    num_rows = hidden_in.shape[0]
-    head_dim = w_k.shape[1]
-    num_heads = w_q.shape[1] // head_dim
-    normed = rms_scale(hidden_in, norm_attn)
-    q_lin = jnp.dot(normed, w_q, preferred_element_type=jnp.float32).reshape(num_rows, num_heads, head_dim)
-    k_lin = jnp.dot(normed, w_k, preferred_element_type=jnp.float32)
-    v_new = jnp.dot(normed, w_v, preferred_element_type=jnp.float32).astype(jnp.bfloat16)
-    cos_t, sin_t = rope_tables(cache_len, head_dim)
-    q_rot = (rotary(q_lin, cos_t[:, None, :], sin_t[:, None, :]) * head_dim ** -0.5).astype(jnp.bfloat16)
-    k_new = rotary(k_lin, cos_t, sin_t).astype(jnp.bfloat16)
-    attn_out = attend(q_rot, k_new, v_new, k_cache, v_cache, cache_len)
-    mixed = jnp.dot(attn_out.reshape(num_rows, num_heads * head_dim), w_o, preferred_element_type=jnp.float32)
-    return hidden_in.astype(jnp.float32) + mixed, k_new, v_new
+def attn_kernel(group, x_ref, len_ref, pos_ref, freq_ref, gain_ref, gain2_ref, k_hbm, v_hbm, wq_hbm, wk_hbm, wv_hbm, wo_hbm,
+                k_ref, v_ref, x1_ref, xn_ref, wq, wkv, wo, kbuf, vbuf, xs, qbuf, obuf, sbuf, knew, vnew,
+                q_sem, kv_sem, o_sem, k_sem, v_sem):
+    rows, width = x_ref.shape
+    dim = wk_hbm.shape[1]
+    heads = wq_hbm.shape[1] // dim
+    ctx = k_hbm.shape[1]
+    slots = kbuf.shape[0]
+    groups = rows // group
+    wide = wo.shape[2]
+    n_out = wo.shape[0]
+
+    def q_load(h):
+        return pltpu.make_async_copy(wq_hbm.at[:, pl.ds(h * dim, dim)], wq.at[h], q_sem.at[h])
+
+    def kv_load(i):
+        return pltpu.make_async_copy((wk_hbm, wv_hbm)[i], wkv.at[i], kv_sem.at[i])
+
+    def o_load(n):
+        return pltpu.make_async_copy(wo_hbm.at[:, pl.ds(n * wide, wide)], wo.at[n], o_sem.at[n])
+
+    def k_load(g):
+        return pltpu.make_async_copy(k_hbm.at[pl.ds(g * group, group)], kbuf.at[lax.rem(g, slots)], k_sem.at[lax.rem(g, slots)])
+
+    def v_load(g):
+        return pltpu.make_async_copy(v_hbm.at[pl.ds(g * group, group)], vbuf.at[lax.rem(g, slots)], v_sem.at[lax.rem(g, slots)])
+
+    kv_load(0).start()
+    kv_load(1).start()
+    for h in range(heads):
+        q_load(h).start()
+    for g in range(slots):
+        k_load(g).start()
+        v_load(g).start()
+    for n in range(n_out):
+        o_load(n).start()
+
+    xw = x_ref[...].astype(jnp.float32)
+    inv = lax.rsqrt(jnp.mean(xw * xw, axis=-1, keepdims=True) + 1e-6)
+    xs[...] = (xw * inv * (1.0 + gain_ref[...].astype(jnp.float32))).astype(jnp.bfloat16)
+    angle = pos_ref[...].astype(jnp.float32) * freq_ref[...]
+    cos_t, sin_t = jnp.cos(angle), jnp.sin(angle)
+    half = dim // 2
+
+    def rotate(t):
+        a, b = t[:, :half], t[:, half:]
+        return a * cos_t - b * sin_t, b * cos_t + a * sin_t
+
+    kv_load(0).wait()
+    ka, kb = rotate(jnp.dot(xs[...], wkv[0], preferred_element_type=jnp.float32))
+    ka, kb = ka.astype(jnp.bfloat16), kb.astype(jnp.bfloat16)
+    k_ref[:, :half] = ka
+    k_ref[:, half:] = kb
+    knew[:, :half] = ka.astype(jnp.float32)
+    knew[:, half:] = kb.astype(jnp.float32)
+    kv_load(1).wait()
+    vv = jnp.dot(xs[...], wkv[1], preferred_element_type=jnp.float32).astype(jnp.bfloat16)
+    v_ref[...] = vv
+    vnew[...] = vv.astype(jnp.float32)
+
+    scale = dim ** -0.5
+    for h in range(heads):
+        q_load(h).wait()
+        qa, qb = rotate(jnp.dot(xs[...], wq[h], preferred_element_type=jnp.float32))
+        qbuf[0, pl.ds(h, rows, stride=heads), :] = (qa * scale).astype(jnp.bfloat16).astype(jnp.float32)
+        qbuf[1, pl.ds(h, rows, stride=heads), :] = (qb * scale).astype(jnp.bfloat16).astype(jnp.float32)
+
+    spots = lax.broadcasted_iota(jnp.int32, (heads, ctx), 1)
+
+    def scores(g):
+        k_load(g).wait()
+        slot = lax.rem(g, slots)
+        for i in range(group):
+            spot = pl.ds(pl.multiple_of((g * group + i) * heads, heads), heads)
+            q = jnp.concatenate([qbuf[0, spot, :], qbuf[1, spot, :]], axis=1).astype(jnp.bfloat16)
+            sbuf[lax.rem(g, 2), i] = lax.dot_general(q, kbuf[slot, i], (((1,), (1,)), ((), ())), preferred_element_type=jnp.float32)
+
+    def values(g):
+        v_load(g).wait()
+        slot = lax.rem(g, slots)
+        for i in range(group):
+            r = g * group + i
+            spot = pl.ds(pl.multiple_of(r * heads, heads), heads)
+            k_row = knew[pl.ds(r, 1), :]
+            v_row = vnew[pl.ds(r, 1), :]
+            new = jnp.sum(qbuf[0, spot, :] * k_row[:, :half] + qbuf[1, spot, :] * k_row[:, half:], axis=1, keepdims=True)
+            valid = spots < len_ref[r]
+            s = jnp.where(valid, sbuf[lax.rem(g, 2), i], -jnp.inf)
+            peak = jnp.maximum(jnp.max(s, axis=1, keepdims=True), new)
+            w = jnp.exp(s - peak)
+            new_w = jnp.exp(new - peak)
+            total = jnp.sum(w, axis=1, keepdims=True) + new_w
+            prob = (w / total).astype(jnp.bfloat16)
+            new_p = (new_w / total).astype(jnp.bfloat16).astype(jnp.float32)
+            o = jnp.dot(prob, vbuf[slot, i], preferred_element_type=jnp.float32)
+            o = o + new_p * v_row
+            obuf[0, spot, :] = o[:, :half]
+            obuf[1, spot, :] = o[:, half:]
+
+    scores(0)
+    k_load(slots).start()
+
+    def body(g, carry):
+        @pl.when(g + 1 < groups)
+        def _():
+            scores(g + 1)
+        values(g)
+        @pl.when(g + slots < groups)
+        def _():
+            v_load(g + slots).start()
+        @pl.when(g + 1 + slots < groups)
+        def _():
+            k_load(g + 1 + slots).start()
+        return carry
+    lax.fori_loop(0, groups, body, 0)
+
+    for h in range(heads):
+        xs[:, h * dim:h * dim + half] = obuf[0, pl.ds(h, rows, stride=heads), :].astype(jnp.bfloat16)
+        xs[:, h * dim + half:(h + 1) * dim] = obuf[1, pl.ds(h, rows, stride=heads), :].astype(jnp.bfloat16)
+
+    def project(n, carry):
+        o_load(n).wait()
+        cols = pl.ds(pl.multiple_of(n * wide, wide), wide)
+        x1_ref[:, cols] = x_ref[:, cols].astype(jnp.float32) + jnp.dot(xs[...], wo[n], preferred_element_type=jnp.float32)
+        return carry
+    lax.fori_loop(0, n_out, project, 0)
+    x1 = x1_ref[...]
+    inv = lax.rsqrt(jnp.mean(x1 * x1, axis=-1, keepdims=True) + 1e-6)
+    xn_ref[...] = (x1 * inv * (1.0 + gain2_ref[...].astype(jnp.float32))).astype(jnp.bfloat16)
+
+
+def attention(hidden_in, k_cache, v_cache, cache_len, norm_attn, norm_mlp, w_q, w_k, w_v, w_o):
+    rows, width = hidden_in.shape
+    ctx, dim = k_cache.shape[1:]
+    heads = w_q.shape[1] // dim
+    group, slots, wide = 8, 4, 512
+    n_out = width // wide
+    sems = pltpu.SemaphoreType.DMA
+    vmem = pl.BlockSpec(memory_space=pltpu.VMEM)
+    smem = pl.BlockSpec(memory_space=pltpu.SMEM)
+    hbm = pl.BlockSpec(memory_space=pl.ANY)
+    freq = 10000.0 ** (-2.0 * jnp.arange(dim // 2, dtype=jnp.float32) / dim)
+    return pl.pallas_call(
+        functools.partial(attn_kernel, group),
+        out_shape=[jax.ShapeDtypeStruct((rows, dim), jnp.bfloat16)] * 2
+        + [jax.ShapeDtypeStruct((rows, width), jnp.float32), jax.ShapeDtypeStruct((rows, width), jnp.bfloat16)],
+        in_specs=[vmem, smem, vmem, vmem, vmem, vmem] + [hbm] * 6,
+        out_specs=[vmem] * 4,
+        scratch_shapes=[
+            pltpu.VMEM((heads, width, dim), jnp.bfloat16),
+            pltpu.VMEM((2, width, dim), jnp.bfloat16),
+            pltpu.VMEM((n_out, heads * dim, wide), jnp.bfloat16),
+            pltpu.VMEM((slots, group, ctx, dim), jnp.bfloat16),
+            pltpu.VMEM((slots, group, ctx, dim), jnp.bfloat16),
+            pltpu.VMEM((rows, width), jnp.bfloat16),
+            pltpu.VMEM((2, rows * heads, dim // 2), jnp.float32),
+            pltpu.VMEM((2, rows * heads, dim // 2), jnp.float32),
+            pltpu.VMEM((2, group, heads, ctx), jnp.float32),
+            pltpu.VMEM((rows, dim), jnp.float32),
+            pltpu.VMEM((rows, dim), jnp.float32),
+            sems((heads,)), sems((2,)), sems((n_out,)), sems((slots,)), sems((slots,)),
+        ],
+        compiler_params=pltpu.CompilerParams(vmem_limit_bytes=60 * 1024 * 1024),
+        cost_estimate=pl.CostEstimate(flops=8 * rows * width * width, bytes_accessed=4 * rows * ctx * dim, transcendentals=0),
+        name='attn',
+    )(hidden_in, cache_len, cache_len[:, None], freq[None], norm_attn[None], norm_mlp[None], k_cache, v_cache, w_q, w_k, w_v, w_o)
 
 
 def mlp_kernel(half, tile, depth_tile, xn_ref, x_ref, wg_hbm, wu_hbm, wd_hbm, out_ref,
@@ -127,7 +243,7 @@
             act = jax.nn.gelu(gate, approximate=True) * lin
             hid[:, pl.ds(pl.multiple_of(n * tile, tile), tile)] = act.astype(jnp.bfloat16)
             return carry
-        lax.fori_loop(0, n_up, body, 0)
+        lax.fori_loop(0, n_up, body, 0, unroll=True)
 
     def exchange(b, n):
         return to(snd.at[b, n], prt.at[b, n], d_send.at[b, n], d_recv.at[b, n], partner)
@@ -155,7 +271,7 @@
             def _():
                 merge(b, n - 1, step)
             return carry
-        lax.fori_loop(0, n_down, body, 0)
+        lax.fori_loop(0, n_down, body, 0, unroll=True)
         merge(b, n_down - 1, step)
 
     gather[0].wait_recv()
@@ -172,15 +288,15 @@
     gather[4].wait_recv()
     gather[8].start()
     down(1, 0)
-    gather[8].wait_recv()
-    up(2)
     gather[5].wait_recv()
     gather[6].wait_recv()
     gather[9].start()
-    down(2, None)
     gather[9].wait_recv()
     up(3)
     down(3, 1)
+    gather[8].wait_recv()
+    up(2)
+    down(2, None)
 
     def relay(n, carry):
         for copy in hops(1, 3, n):
@@ -257,8 +373,7 @@
     full_mat = P(None, None)
 
     def per_device(hidden_in, k_cache, v_cache, cache_len, norm_attn, norm_mlp, w_q, w_k, w_v, w_o, w_gate, w_up, w_down):
-        x_mid, k_new, v_new = attention_block(hidden_in, k_cache, v_cache, cache_len, norm_attn, w_q, w_k, w_v, w_o)
-        xn_mid = rms_scale(x_mid, norm_mlp)
+        k_new, v_new, x_mid, xn_mid = attention(hidden_in, k_cache, v_cache, cache_len, norm_attn, norm_mlp, w_q, w_k, w_v, w_o)
         return mlp(xn_mid, x_mid, w_gate, w_up, w_down), k_new, v_new
 
     return jax.shard_map(

time: 109 us -> 99.2 us (0.910)
  matrix products: 28.2 us -> 0 us
  Pallas kernels: 71.4 us -> 91.9 us
  other arithmetic: 5.41 us -> 0.55 us
  local copies, waits for them, and re-layouts: 2.88 us -> 5.84 us
    pallas_call x0 -> x1, Pallas kernels: none -> 28.9 us  [attention(): pl.pallas_call(functools.partial(attn_kernel, group), out_shape=[jax.Shap...]
    dot_general x7 -> x0, matrix products: 28.2 us -> none  [the longest x1 10.5 us: attend(): jnp.einsum('bhd,btd->bht', q_rot, k_cache, preferred_element_type=jnp.flo...]
    pallas_call x1, Pallas kernels: 71.4 us -> 63 us  [mlp(): pl.pallas_call(functools.partial(mlp_kernel, rows // 2, tile, depth_tile)...]
    broadcast_in_dim x0 -> x3, local copies, waits for them, and re-layouts: none -> 3.96 us  [the longest x1 1.39 us: attention(): cache_len[:, None]]
    convert_element_type x2 -> x0, other arithmetic: 1.76 us -> none  [the longest x1 1.1 us: rms_scale(): (wide_vals * inv_rms * (1.0 + gain_vec.astype(jnp.float32))).astype(jnp.b...]
    reduce_sum x2 -> x0, other arithmetic: 1.59 us -> none  [the longest x1 1.23 us: rms_scale(): jnp.mean(wide_vals * wide_vals, axis=-1, keepdims=True) + 1e-06]
    unnamed x21 -> x1, local copies, waits for them, and re-layouts: 2.88 us -> 1.88 us
where the time goes in v2:
time: 99.2 us; the launch traced here: 98.9 us
  Pallas kernels  91.9 us (93%)
  local copies, waits for them, and re-layouts  5.84 us (6%)
    pallas_call x1, Pallas kernels, mlp(): pl.pallas_call(functools.partial(mlp_kernel, rows // 2, tile, depth_tile)...  63 us
    pallas_call x1, Pallas kernels, attention(): pl.pallas_call(functools.partial(attn_kernel, group), out_shape=[jax.Shap...  28.9 us

profile of v2, /device:TPU:81, one launch (start us, length us, event | category | flops | bytes accessed | tf_op | source)
XLA Modules:
  0.0 98.9 jit_solution(9185748584273095657)
XLA Ops:
  0.6 0.5 multiply_power_fusion.freq_ref
  1.2 1.3 %broadcast_in_dim.11.gain_ref = bf16[1,2048]{1,0:T(2,128)(2,1)} reshape(bf16[2048]{0:T(1024)(128)(2,1)} %param.17) | data formatting | bytes 8192 | tf_op jit(solution)/shard_map/broadcast_in_dim | solution.py:178
  2.5 1.3 %broadcast_in_dim.12.gain2_ref = bf16[1,2048]{1,0:T(2,128)(2,1)} reshape(bf16[2048]{0:T(1024)(128)(2,1)} %param.18) | data formatting | bytes 8192 | tf_op jit(solution)/shard_map/broadcast_in_dim | solution.py:178
  3.7 1.4 %copy.16.pos_ref = s32[128,1]{1,0:T(8,128)} copy(s32[128,1]{0,1:T(1,128)} %bitcast.1) | data formatting | bytes 1024 | tf_op jit(solution)/shard_map/broadcast_in_dim | solution.py:178
  5.1 28.9 %attn.1 = (bf16[128,256]{1,0:T(8,128)(2,1)}, bf16[128,256]{1,0:T(8,128)(2,1)}, f32[128,2048]{1,0:T(8,128)}, bf16[128,2048]{1,0:T(8,128)(2,1)}) custom-call(bf16[128,2048]{1,0:T(8,128)(2,1)} %x_ref.1, s32[128]{0:T(128)} %len_ref.1, s32[128,1]{1,0:T(8,128)} %copy.16.pos_ref, f32[1,128]{1,0:T(1,128)} %multiply_power_fusion.freq_ref, ...), custom_call_target="tpu_custom_call" | custom-call | flops 4294967296 | bytes 33554432 | tf_op jit(solution)/shard_map/attn/pallas_call | solution.py:155
  34.0 63.0 %mlp.1 = bf16[128,2048]{1,0:T(8,128)(2,1)} custom-call(bf16[128,2048]{1,0:T(8,128)(2,1)} %get-tuple-element.7.xn_ref, f32[128,2048]{1,0:T(8,128)} %get-tuple-element.8.x_ref, bf16[2048,2048]{1,0:T(8,128)(2,1)} %wg_hbm.1, bf16[2048,2048]{1,0:T(8,128)(2,1)} %wu_hbm.1, bf16[2048,2048]{1,0:T(8,128)(2,1)} %wd_hbm.1), custom_call_target="tpu_custom_call" | custom-call | flops 25769803776 | bytes 25165824 | tf_op jit(solution)/shard_map/mlp/pallas_call | solution.py:343
  97.1 1.9 %copy.18 = bf16[128,2048]{1,0:T(8,128)(2,1)} copy(bf16[128,2048]{1,0:T(8,128)(2,1)} %mlp.1) | data formatting | bytes 1048576

commit v3 on v0

v3 whole, which is shorter than its diff:
```python
import functools

import jax
import jax.numpy as jnp
import numpy as np
from jax import lax
from jax.experimental import pallas as pl
from jax.experimental.pallas import tpu as pltpu
from jax.sharding import PartitionSpec as P

MESH = pl.DeviceIdType.MESH


def layer_kernel(group, x_ref, len_ref, freq_ref, gain_ref, gain2_ref, k_hbm, v_hbm, wq_hbm, wk_hbm, wv_hbm, wo_hbm,
                 wg_hbm, wu_hbm, wd_hbm, out_ref, k_ref, v_ref,
                 wg, wu, wd, wkv, kbuf, vbuf, xs, qbuf, obuf, sbuf, knew, vnew, turn, x1, xb, hid, own, snd, prt, ring,
                 w_sem, q_sem, kv_sem, o_sem, k_sem, v_sem, ag_send, ag_recv, d_send, d_recv, r_send, r_recv):
    chips = lax.axis_size('tp') // 2
    me = lax.axis_index('tp')
    core = lax.rem(me, 2)
    chip = me // 2
    partner = me + 1 - 2 * core
    ahead = 2 * lax.rem(chip + 1, chips) + core
    behind = 2 * lax.rem(chip + chips - 1, chips) + core

    rows, width = x_ref.shape
    dim = wk_hbm.shape[1]
    heads = wq_hbm.shape[1] // dim
    ctx = k_hbm.shape[1]
    slots = kbuf.shape[0]
    groups = rows // group
    n_tile, _, tile = wg.shape
    side = rows // 2
    quart = rows // 4
    half = dim // 2
    per_part = groups // 2
    per_side = per_part // 2

    barrier = pltpu.get_barrier_semaphore()
    for dev in (partner, ahead, behind):
        pl.semaphore_signal(barrier, inc=1, device_id={'tp': dev}, device_id_type=MESH)

    def fetch(hbm, buf, n, sem):
        return pltpu.make_async_copy(hbm.at[:, pl.ds(pl.multiple_of(n * tile, tile), tile)], buf.at[n], sem)

    def q_load(n):
        return fetch(wq_hbm, wd, n, q_sem.at[n])

    def o_load(n):
        return fetch(wo_hbm, wu, n, o_sem.at[n])

    def gate_load(n):
        return fetch(wg_hbm, wg, n, w_sem.at[0, n])

    def up_load(n):
        return fetch(wu_hbm, wu, n, w_sem.at[1, n])

    def down_load(n):
        return fetch(wd_hbm, wd, n, w_sem.at[2, n])

    def kv_load(i):
        return pltpu.make_async_copy((wk_hbm, wv_hbm)[i], wkv.at[i], kv_sem.at[i])

    def first_row(g):
        j = lax.rem(g, per_part)
        return pl.multiple_of((j // per_side) * side + (g // per_part) * quart + lax.rem(j, per_side) * group, group)

    def k_load(g):
        slot = lax.rem(g, slots)
        return pltpu.make_async_copy(k_hbm.at[pl.ds(first_row(g), group)], kbuf.at[slot], k_sem.at[slot])

    def v_load(g):
        slot = lax.rem(g, slots)
        return pltpu.make_async_copy(v_hbm.at[pl.ds(first_row(g), group)], vbuf.at[slot], v_sem.at[slot])

    def to(src, dst, send, recv, dev):
        return pltpu.make_async_remote_copy(src_ref=src, dst_ref=dst, send_sem=send, recv_sem=recv,
                                            device_id={'tp': dev}, device_id_type=MESH)

    kv_load(0).start()
    kv_load(1).start()
    for n in range(n_tile):
        q_load(n).start()

    xw = x_ref[...].astype(jnp.float32)
    inv = lax.rsqrt(jnp.mean(xw * xw, axis=-1, keepdims=True) + 1e-6)
    xs[...] = (xw * inv * (1.0 + gain_ref[...].astype(jnp.float32)[None])).astype(jnp.bfloat16)
    for r in range(rows):
        turn[pl.ds(r, 1), :] = len_ref[r].astype(jnp.float32) * freq_ref[...]
    angle = turn[...]
    cos_t, sin_t = jnp.cos(angle), jnp.sin(angle)

    def rotate(a, b):
        return a * cos_t - b * sin_t, b * cos_t + a * sin_t

    kv_load(0).wait()
    kk = jnp.dot(xs[...], wkv[0], preferred_element_type=jnp.float32)
    ka, kb = rotate(kk[:, :half], kk[:, half:])
    ka, kb = ka.astype(jnp.bfloat16), kb.astype(jnp.bfloat16)
    k_ref[:, :half] = ka
    k_ref[:, half:] = kb
    knew[:, :half] = ka.astype(jnp.float32)
    knew[:, half:] = kb.astype(jnp.float32)
    kv_load(1).wait()
    vv = jnp.dot(xs[...], wkv[1], preferred_element_type=jnp.float32).astype(jnp.bfloat16)
    v_ref[...] = vv
    vnew[...] = vv.astype(jnp.float32)

    scale = dim ** -0.5
    for n in range(n_tile):
        q_load(n).wait()
        if n < slots:
            k_load(n).start()
            v_load(n).start()
        ql = jnp.dot(xs[...], wd[n], preferred_element_type=jnp.float32)
        for i in range(tile // dim):
            h = n * (tile // dim) + i
            qa, qb = rotate(ql[:, i * dim:i * dim + half], ql[:, i * dim + half:(i + 1) * dim])
            qbuf[0, pl.ds(h, rows, stride=heads), :] = (qa * scale).astype(jnp.bfloat16).astype(jnp.float32)
            qbuf[1, pl.ds(h, rows, stride=heads), :] = (qb * scale).astype(jnp.bfloat16).astype(jnp.float32)
    for n in range(n_tile):
        o_load(n).start()

    spots = lax.broadcasted_iota(jnp.int32, (heads, ctx), 1)

    def scores(g):
        slot = lax.rem(g, slots)
        base = first_row(lax.rem(g, groups))
        for i in range(group):
            spot = pl.ds(pl.multiple_of((base + i) * heads, heads), heads)
            q = jnp.concatenate([qbuf[0, spot, :], qbuf[1, spot, :]], axis=1).astype(jnp.bfloat16)
            sbuf[lax.rem(g, 2), i] = lax.dot_general(q, kbuf[slot, i], (((1,), (1,)), ((), ())), preferred_element_type=jnp.float32)

    def values(g):
        slot = lax.rem(g, slots)
        base = first_row(g)
        for i in range(group):
            r = base + i
            spot = pl.ds(pl.multiple_of(r * heads, heads), heads)
            k_row = knew[pl.ds(r, 1), :]
            v_row = vnew[pl.ds(r, 1), :]
            new = jnp.sum(qbuf[0, spot, :] * k_row[:, :half] + qbuf[1, spot, :] * k_row[:, half:], axis=1, keepdims=True)
            valid = spots < len_ref[r]
            s = jnp.where(valid, sbuf[lax.rem(g, 2), i], -jnp.inf)
            peak = jnp.maximum(jnp.max(s, axis=1, keepdims=True), new)
            w = jnp.exp(s - peak)
            new_w = jnp.exp(new - peak)
            total = jnp.sum(w, axis=1, keepdims=True) + new_w
            prob = (w / total).astype(jnp.bfloat16)
            new_p = (new_w / total).astype(jnp.bfloat16).astype(jnp.float32)
            o = jnp.dot(prob, vbuf[slot, i], preferred_element_type=jnp.float32) + new_p * v_row
            to_spot = pl.ds(pl.multiple_of((lax.rem(g, per_part) * group + i) * heads, heads), heads)
            obuf[0, to_spot, :] = o[:, :half]
            obuf[1, to_spot, :] = o[:, half:]

    def attend(g, carry):
        @pl.when(g + 1 < groups)
        def _():
            k_load(g + 1).wait()
        v_load(g).wait()
        scores(g + 1)
        values(g)
        @pl.when(g + slots < groups)
        def _():
            v_load(g + slots).start()
        @pl.when(g + 1 + slots < groups)
        def _():
            k_load(g + 1 + slots).start()
        @pl.when(g >= groups - n_tile)
        def _():
            gate_load(g - (groups - n_tile)).start()
        return carry

    def finish(s):
        for h in range(heads):
            spot = pl.ds(h, side, stride=heads)
            xs[0:side, h * dim:h * dim + half] = obuf[0, spot, :].astype(jnp.bfloat16)
            xs[0:side, h * dim + half:(h + 1) * dim] = obuf[1, spot, :].astype(jnp.bfloat16)
        a, b = pl.ds(s * quart, quart), pl.ds(side + s * quart, quart)

        def project(n, carry):
            if s == 0:
                o_load(n).wait()
            cols = pl.ds(pl.multiple_of(n * tile, tile), tile)
            mixed = jnp.dot(xs[0:side, :], wu[n], preferred_element_type=jnp.float32)
            x1[a, cols] = x_ref[a, cols].astype(jnp.float32) + mixed[0:quart]
            x1[b, cols] = x_ref[b, cols].astype(jnp.float32) + mixed[quart:side]
            if s == 1:
                up_load(n).start()
            return carry
        lax.fori_loop(0, n_tile, project, 0)
        for j, part in ((0, a), (1, b)):
            mid = x1[part, :]
            inv = lax.rsqrt(jnp.mean(mid * mid, axis=-1, keepdims=True) + 1e-6)
            normed = (mid * inv * (1.0 + gain2_ref[...].astype(jnp.float32)[None])).astype(jnp.bfloat16)
            xb[2 * s + 1, side + j * quart:side + (j + 1) * quart, :] = normed

    def span(i, n=1):
        return pl.ds(i * quart, n * quart)

    def gather(s, i):
        near, far = 2 * s, 2 * s + 1
        src, dst, dev = (
            (xb.at[far, span(2)], xb.at[near, span(1)], ahead),
            (xb.at[far, span(3)], xb.at[near, span(3)], ahead),
            (xb.at[far, span(3)], xb.at[near, span(0)], behind),
            (xb.at[far, span(2)], xb.at[near, span(2)], behind),
            (xb.at[near, span(1)], xb.at[far, span(0)], ahead),
            (xb.at[near, span(0)], xb.at[far, span(1)], behind),
            (xb.at[near, span(0, 2)], xb.at[near, span(4, 2)], partner),
            (xb.at[near, span(2, 2)], xb.at[near, span(6, 2)], partner),
            (xb.at[far, span(0, 4)], xb.at[far, span(4, 4)], partner),
        )[i]
        return to(src, dst, ag_send.at[s, i], ag_recv.at[s, i], dev)

    def send(s):
        for i in (0, 2, 1, 3):
            gather(s, i).start()

    def arrive(s, *ids):
        for i in ids:
            gather(s, i).wait_recv()

    def forward(s):
        arrive(s, 0, 2)
        for i in (4, 5, 6):
            gather(s, i).start()

    k_load(0).wait()
    scores(0)
    k_load(slots).start()
    lax.fori_loop(0, per_part, attend, 0)
    finish(0)
    pl.semaphore_wait(barrier, 3)
    send(0)
    lax.fori_loop(per_part, groups, attend, 0)
    forward(0)
    finish(1)
    for n in range(n_tile):
        down_load(n).start()
    send(1)

    def up_step(b, n):
        if b == 0:
            gate_load(n).wait()
            up_load(n).wait()
        gate = jnp.dot(xb[b], wg[n], preferred_element_type=jnp.float32)
        lin = jnp.dot(xb[b], wu[n], preferred_element_type=jnp.float32)
        hid[:, n * tile:(n + 1) * tile] = (jax.nn.gelu(gate, approximate=True) * lin).astype(jnp.bfloat16)

    def swap(b, n):
        return to(snd.at[b, n], prt.at[b, n], d_send.at[b, n], d_recv.at[b, n], partner)

    def hops(s, step, n):
        b = (2 * s, 2 * s + 1, 2 * s)[step]
        fwd = (0, 0, 2)[step]
        return (to(own.at[b, n, span(fwd)], ring.at[s, step, n, span(0)], r_send.at[s, step, 0, n], r_recv.at[s, step, 0, n], ahead),
                to(own.at[b, n, span(fwd + 1)], ring.at[s, step, n, span(1)], r_send.at[s, step, 1, n], r_recv.at[s, step, 1, n], behind))

    def merge(b, n):
        swap(b, n).wait_recv()
        own[b, n] = own[b, n] + prt[b, n]
        for copy in hops(b // 2, b % 2, n):
            copy.start()

    def down(b):
        for n in range(n_tile):
            if b == 0:
                down_load(n).wait()
            part = jnp.dot(hid[...], wd[n], preferred_element_type=jnp.float32)
            own[b, n] = part[0:rows]
            snd[b, n] = part[rows:2 * rows]
            swap(b, n).start()
            if n > 0:
                merge(b, n - 1)
        merge(b, n_tile - 1)

    def relay(s, n):
        for copy in hops(s, 1, n):
            copy.wait_recv()
        own[2 * s, n, span(2, 2)] = own[2 * s, n, span(2, 2)] + ring[s, 1, n]
        for copy in hops(s, 2, n):
            copy.start()

    def settle(s, n):
        for step in (0, 2):
            for copy in hops(s, step, n):
                copy.wait_recv()
        cols = slice(n * tile, (n + 1) * tile)
        a, b = pl.ds(s * quart, quart), pl.ds(side + s * quart, quart)
        far = 2 * s + 1
        out_ref[a, cols] = (x1[a, cols] + (own[far, n, span(2)] + (ring[s, 0, n, span(1)] + ring[s, 2, n, span(0)]))).astype(jnp.bfloat16)
        out_ref[b, cols] = (x1[b, cols] + (own[far, n, span(3)] + (ring[s, 0, n, span(0)] + ring[s, 2, n, span(1)]))).astype(jnp.bfloat16)

    arrive(0, 1, 3)
    gather(0, 7).start()
    arrive(0, 6, 7)
    for n in range(n_tile):
        up_step(0, n)
    forward(1)
    arrive(0, 4, 5)
    gather(0, 8).start()
    down(0)
    arrive(1, 1, 3)
    gather(1, 7).start()
    arrive(0, 8)
    for n in range(n_tile):
        up_step(1, n)
    down(1)
    arrive(1, 4, 5)
    gather(1, 8).start()
    arrive(1, 6, 7)
    for n in range(n_tile):
        up_step(2, n)
        relay(0, n)
    down(2)
    arrive(1, 8)
    for n in range(n_tile):
        up_step(3, n)
    down(3)
    for n in range(n_tile):
        settle(0, n)
    for n in range(n_tile):
        relay(1, n)
    for n in range(n_tile):
        settle(1, n)

    for s in range(2):
        for i in range(9):
            gather(s, i).wait_send()

    def drain(n, carry):
        for b in range(4):
            swap(b, n).wait_send()
        for s in range(2):
            for step in range(3):
                for copy in hops(s, step, n):
                    copy.wait_send()
        return carry
    lax.fori_loop(0, n_tile, drain, 0)


def layer(hidden_in, k_cache, v_cache, cache_len, norm_attn, norm_mlp, w_q, w_k, w_v, w_o, w_gate, w_up, w_down):
    rows, width = hidden_in.shape
    ctx, dim = k_cache.shape[1:]
    heads = w_q.shape[1] // dim
    units = w_gate.shape[1]
    group, slots, tile = 8, 4, 512
    n_tile = width // tile
    assert heads * dim == width and units == width
    sems = pltpu.SemaphoreType.DMA
    bf16, f32 = jnp.bfloat16, jnp.float32
    vmem = pl.BlockSpec(memory_space=pltpu.VMEM)
    smem = pl.BlockSpec(memory_space=pltpu.SMEM)
    hbm = pl.BlockSpec(memory_space=pl.ANY)
    freq = np.float32(10000.0 ** (-2.0 * np.arange(dim // 2) / dim))[None]
    return pl.pallas_call(
        functools.partial(layer_kernel, group),
        out_shape=[jax.ShapeDtypeStruct((rows, width), bf16)] + [jax.ShapeDtypeStruct((rows, dim), bf16)] * 2,
        in_specs=[vmem, smem, vmem, vmem, vmem] + [hbm] * 9,
        out_specs=[vmem] * 3,
        scratch_shapes=[
            pltpu.VMEM((n_tile, width, tile), bf16),
            pltpu.VMEM((n_tile, width, tile), bf16),
            pltpu.VMEM((n_tile, units, tile), bf16),
            pltpu.VMEM((2, width, dim), bf16),
            pltpu.VMEM((slots, group, ctx, dim), bf16),
            pltpu.VMEM((slots, group, ctx, dim), bf16),
            pltpu.VMEM((rows, width), bf16),
            pltpu.VMEM((2, rows * heads, dim // 2), f32),
            pltpu.VMEM((2, rows * heads // 2, dim // 2), f32),
            pltpu.VMEM((2, group, heads, ctx), f32),
            pltpu.VMEM((rows, dim), f32),
            pltpu.VMEM((rows, dim), f32),
            pltpu.VMEM((rows, dim // 2), f32),
            pltpu.VMEM((rows, width), f32),
            pltpu.VMEM((4, 2 * rows, width), bf16),
            pltpu.VMEM((2 * rows, units), bf16),
            pltpu.VMEM((4, n_tile, rows, tile), f32),
            pltpu.VMEM((4, n_tile, rows, tile), f32),
            pltpu.VMEM((4, n_tile, rows, tile), f32),
            pltpu.VMEM((2, 3, n_tile, rows // 2, tile), f32),
            sems((3, n_tile)), sems((n_tile,)), sems((2,)), sems((n_tile,)), sems((slots,)), sems((slots,)),
            sems((2, 9)), sems((2, 9)),
            sems((4, n_tile)), sems((4, n_tile)),
            sems((2, 3, 2, n_tile)), sems((2, 3, 2, n_tile)),
        ],
        compiler_params=pltpu.CompilerParams(collective_id=0, has_side_effects=True, vmem_limit_bytes=63 * 1024 * 1024),
        cost_estimate=pl.CostEstimate(flops=48 * rows * width * units, bytes_accessed=4 * rows * ctx * dim + 10 * width * width, transcendentals=0),
        name='layer',
    )(hidden_in, cache_len, freq, norm_attn, norm_mlp, k_cache, v_cache, w_q, w_k, w_v, w_o, w_gate, w_up, w_down)


def solution(mesh):
    row_spec = P(('dp', 'tp'), None)
    cache_spec = P(('dp', 'tp'), None, None)
    full_vec = P(None)
    full_mat = P(None, None)

    return jax.shard_map(
        layer,
        mesh=mesh,
        in_specs=(row_spec, cache_spec, cache_spec, P(('dp', 'tp')), full_vec, full_vec,
                  full_mat, full_mat, full_mat, full_mat, P(None, 'tp'), P(None, 'tp'), P('tp', None)),
        out_specs=(row_spec, row_spec, row_spec),
        check_vma=False,
    )
```

time: 180 us -> 88.6 us (0.49)
  Pallas kernels: 0 us -> 82.9 us
  waiting for transfers between devices: 81.3 us -> 0 us
  matrix products: 74.4 us -> 0 us
  between operations: 14.2 us -> 0.65 us
  other arithmetic: 8.7 us -> 0 us
  local copies, waits for them, and re-layouts: 0.5 us -> 4.83 us
    pallas_call x0 -> x1, Pallas kernels: none -> 82.9 us  [layer(): pl.pallas_call(functools.partial(layer_kernel, group), out_shape=[jax.Sha...]
    dot_general x9 -> x0, matrix products: 74.4 us -> none  [the longest x1 31 us: per_device(): part_sum = jnp.dot(hidden_act, w_down, preferred_element_type=jnp.float32)]
    reduce_scatter x1 -> x0, waiting for transfers between devices: 48 us -> none  [per_device(): down_sum = lax.psum_scatter(part_sum, 'tp', scatter_dimension=0, tiled=True)]
    all_gather x1 -> x0, waiting for transfers between devices: 33.2 us -> none  [per_device(): group_rows = lax.all_gather(xn_mid, 'tp', axis=0, tiled=True)]
    unnamed x12 -> x3, local copies, waits for them, and re-layouts: 0.5 us -> 4.83 us
    convert_element_type x3 -> x0, other arithmetic: 3.82 us -> none  [the longest x1 2.12 us: per_device(): return ((x_mid + down_sum).astype(jnp.bfloat16), k_new, v_new)]
  transfers between devices with their start and end apart: 2 -> 0, of which waited for: 2 -> 0; matrix products, arithmetic and copies ran while one was open for 0% -> 0% of each run, Pallas kernels for 0% -> 0%
where the time goes in v3:
time: 88.6 us; the launch traced here: 88.4 us
  Pallas kernels  82.9 us (94%)
  local copies, waits for them, and re-layouts  4.83 us (5%)
    pallas_call x1, Pallas kernels, layer(): pl.pallas_call(functools.partial(layer_kernel, group), out_shape=[jax.Sha...  82.9 us
    unnamed x3, local copies, waits for them, and re-layouts  4.83 us

profile of v3, /device:TPU:81, one launch (start us, length us, event | category | flops | bytes accessed | tf_op | source)
XLA Modules:
  0.0 88.4 jit_solution(4809561732437569452)
XLA Ops:
  0.6 82.9 %layer.1 = (bf16[128,2048]{1,0:T(8,128)(2,1)}, bf16[128,256]{1,0:T(8,128)(2,1)}, bf16[128,256]{1,0:T(8,128)(2,1)}) custom-call(bf16[128,2048]{1,0:T(8,128)(2,1)} %x_ref.1, s32[128]{0:T(128)} %len_ref.1, f32[1,128]{1,0:T(1,128)} %constant.2.clone.freq_ref, bf16[2048]{0:T(1024)(128)(2,1)} %gain_ref.1, bf16[2048]{0:T(1024)(128)(2,1)} %gain2_ref.1, ...), custom_call_target="tpu_custom_call" | custom-call | flops 25769803776 | bytes 75497472 | tf_op jit(solution)/shard_map/layer/pallas_call | solution.py:357
  83.6 1.9 %copy.20 = bf16[128,2048]{1,0:T(8,128)(2,1)} copy(bf16[128,2048]{1,0:T(8,128)(2,1)} %get-tuple-element.6) | data formatting | bytes 1048576
  85.5 1.5 %copy.21 = bf16[128,256]{1,0:T(8,128)(2,1)} copy(bf16[128,256]{1,0:T(8,128)(2,1)} %get-tuple-element.7) | data formatting | bytes 131072
  86.9 1.5 %copy.22 = bf16[128,256]{1,0:T(8,128)(2,1)} copy(bf16[128,256]{1,0:T(8,128)(2,1)} %get-tuple-element.8) | data formatting | bytes 131072

commit v4 on v3

--- a/solution.py
+++ b/solution.py
@@ -11,10 +11,10 @@
 MESH = pl.DeviceIdType.MESH
 
 
-def layer_kernel(group, x_ref, len_ref, freq_ref, gain_ref, gain2_ref, k_hbm, v_hbm, wq_hbm, wk_hbm, wv_hbm, wo_hbm,
-                 wg_hbm, wu_hbm, wd_hbm, out_ref, k_ref, v_ref,
-                 wg, wu, wd, wkv, kbuf, vbuf, xs, qbuf, obuf, sbuf, knew, vnew, turn, x1, xb, hid, own, snd, prt, ring,
-                 w_sem, q_sem, kv_sem, o_sem, k_sem, v_sem, ag_send, ag_recv, d_send, d_recv, r_send, r_recv):
+def layer_kernel(group, x_hbm, len_hbm, freq_hbm, gain_hbm, gain2_hbm, k_hbm, v_hbm, wq_hbm, wk_hbm, wv_hbm, wo_hbm,
+                 wg_hbm, wu_hbm, wd_hbm, out_hbm, k_out, v_out,
+                 x_ref, len_ref, freq_ref, gain_ref, gain2_ref, out_ref, k_ref, v_ref, wg, wu, wd, wkv, kbuf, vbuf, xs, qbuf, obuf, sbuf, knew, vnew, turn, x1, xb, hid, own, snd, prt, ring,
+                 x_sem, y_sem, w_sem, q_sem, kv_sem, o_sem, k_sem, v_sem, ag_send, ag_recv, d_send, d_recv, r_send, r_recv):
     chips = lax.axis_size('tp') // 2
     me = lax.axis_index('tp')
     core = lax.rem(me, 2)
@@ -77,11 +77,20 @@
         return pltpu.make_async_remote_copy(src_ref=src, dst_ref=dst, send_sem=send, recv_sem=recv,
                                             device_id={'tp': dev}, device_id_type=MESH)
 
+    small = [pltpu.make_async_copy(src, dst, x_sem.at[i]) for i, (src, dst) in enumerate(
+        ((x_hbm, x_ref), (gain_hbm, gain_ref), (len_hbm, len_ref), (freq_hbm, freq_ref), (gain2_hbm, gain2_ref)))]
+    for copy in small:
+        copy.start()
     kv_load(0).start()
     kv_load(1).start()
     for n in range(n_tile):
         q_load(n).start()
-
+    for g in range(slots):
+        k_load(g).start()
+        v_load(g).start()
+
+    for copy in small:
+        copy.wait()
     xw = x_ref[...].astype(jnp.float32)
     inv = lax.rsqrt(jnp.mean(xw * xw, axis=-1, keepdims=True) + 1e-6)
     xs[...] = (xw * inv * (1.0 + gain_ref[...].astype(jnp.float32)[None])).astype(jnp.bfloat16)
@@ -105,21 +114,19 @@
     vv = jnp.dot(xs[...], wkv[1], preferred_element_type=jnp.float32).astype(jnp.bfloat16)
     v_ref[...] = vv
     vnew[...] = vv.astype(jnp.float32)
+    outs = [pltpu.make_async_copy(k_ref, k_out, y_sem.at[0]), pltpu.make_async_copy(v_ref, v_out, y_sem.at[1])]
+    for copy in outs:
+        copy.start()
 
     scale = dim ** -0.5
     for n in range(n_tile):
         q_load(n).wait()
-        if n < slots:
-            k_load(n).start()
-            v_load(n).start()
         ql = jnp.dot(xs[...], wd[n], preferred_element_type=jnp.float32)
         for i in range(tile // dim):
             h = n * (tile // dim) + i
             qa, qb = rotate(ql[:, i * dim:i * dim + half], ql[:, i * dim + half:(i + 1) * dim])
             qbuf[0, pl.ds(h, rows, stride=heads), :] = (qa * scale).astype(jnp.bfloat16).astype(jnp.float32)
             qbuf[1, pl.ds(h, rows, stride=heads), :] = (qb * scale).astype(jnp.bfloat16).astype(jnp.float32)
-    for n in range(n_tile):
-        o_load(n).start()
 
     spots = lax.broadcasted_iota(jnp.int32, (heads, ctx), 1)
 
@@ -166,6 +173,9 @@
         @pl.when(g + 1 + slots < groups)
         def _():
             k_load(g + 1 + slots).start()
+        @pl.when(g < n_tile)
+        def _():
+            o_load(g).start()
         @pl.when(g >= groups - n_tile)
         def _():
             gate_load(g - (groups - n_tile)).start()
@@ -189,6 +199,9 @@
                 up_load(n).start()
             return carry
         lax.fori_loop(0, n_tile, project, 0)
+        if s == 1:
+            arrive(0, 1, 3)
+            gather(0, 7).start()
         for j, part in ((0, a), (1, b)):
             mid = x1[part, :]
             inv = lax.rsqrt(jnp.mean(mid * mid, axis=-1, keepdims=True) + 1e-6)
@@ -263,6 +276,19 @@
         for copy in hops(b // 2, b % 2, n):
             copy.start()
 
+    pending = []
+
+    def flush(keep=0):
+        while len(pending) > keep:
+            merge(*pending.pop(0))
+
+    def up(b, after=None):
+        for n in range(n_tile):
+            up_step(b, n)
+            flush()
+            if after is not None:
+                after(n)
+
     def down(b):
         for n in range(n_tile):
             if b == 0:
@@ -271,9 +297,8 @@
             own[b, n] = part[0:rows]
             snd[b, n] = part[rows:2 * rows]
             swap(b, n).start()
-            if n > 0:
-                merge(b, n - 1)
-        merge(b, n_tile - 1)
+            pending.append((b, n))
+            flush(2)
 
     def relay(s, n):
         for copy in hops(s, 1, n):
@@ -292,11 +317,15 @@
         out_ref[a, cols] = (x1[a, cols] + (own[far, n, span(2)] + (ring[s, 0, n, span(1)] + ring[s, 2, n, span(0)]))).astype(jnp.bfloat16)
         out_ref[b, cols] = (x1[b, cols] + (own[far, n, span(3)] + (ring[s, 0, n, span(0)] + ring[s, 2, n, span(1)]))).astype(jnp.bfloat16)
 
-    arrive(0, 1, 3)
-    gather(0, 7).start()
+    def give(s):
+        a, b = pl.ds(s * quart, quart), pl.ds(side + s * quart, quart)
+        for j, part in enumerate((a, b)):
+            copy = pltpu.make_async_copy(out_ref.at[part], out_hbm.at[part], y_sem.at[2 + 2 * s + j])
+            copy.start()
+            outs.append(copy)
+
     arrive(0, 6, 7)
-    for n in range(n_tile):
-        up_step(0, n)
+    up(0)
     forward(1)
     arrive(0, 4, 5)
     gather(0, 8).start()
@@ -304,26 +333,27 @@
     arrive(1, 1, 3)
     gather(1, 7).start()
     arrive(0, 8)
-    for n in range(n_tile):
-        up_step(1, n)
+    up(1)
     down(1)
     arrive(1, 4, 5)
     gather(1, 8).start()
     arrive(1, 6, 7)
-    for n in range(n_tile):
-        up_step(2, n)
-        relay(0, n)
+    up(2, lambda n: relay(0, n))
     down(2)
     arrive(1, 8)
-    for n in range(n_tile):
-        up_step(3, n)
+    up(3)
     down(3)
-    for n in range(n_tile):
+    settle(0, 0)
+    settle(0, 1)
+    flush()
+    for n in range(2, n_tile):
         settle(0, n)
+    give(0)
     for n in range(n_tile):
         relay(1, n)
     for n in range(n_tile):
         settle(1, n)
+    give(1)
 
     for s in range(2):
         for i in range(9):
@@ -338,6 +368,8 @@
                     copy.wait_send()
         return carry
     lax.fori_loop(0, n_tile, drain, 0)
+    for copy in outs:
+        copy.wait()
 
 
 def layer(hidden_in, k_cache, v_cache, cache_len, norm_attn, norm_mlp, w_q, w_k, w_v, w_o, w_gate, w_up, w_down):
@@ -350,16 +382,22 @@
     assert heads * dim == width and units == width
     sems = pltpu.SemaphoreType.DMA
     bf16, f32 = jnp.bfloat16, jnp.float32
-    vmem = pl.BlockSpec(memory_space=pltpu.VMEM)
-    smem = pl.BlockSpec(memory_space=pltpu.SMEM)
     hbm = pl.BlockSpec(memory_space=pl.ANY)
     freq = np.float32(10000.0 ** (-2.0 * np.arange(dim // 2) / dim))[None]
-    return pl.pallas_call(
+    results = pl.pallas_call(
         functools.partial(layer_kernel, group),
         out_shape=[jax.ShapeDtypeStruct((rows, width), bf16)] + [jax.ShapeDtypeStruct((rows, dim), bf16)] * 2,
-        in_specs=[vmem, smem, vmem, vmem, vmem] + [hbm] * 9,
-        out_specs=[vmem] * 3,
+        in_specs=[hbm] * 14,
+        out_specs=[hbm] * 3,
         scratch_shapes=[
+            pltpu.VMEM((rows, width), bf16),
+            pltpu.SMEM((rows,), jnp.int32),
+            pltpu.VMEM((1, dim // 2), f32),
+            pltpu.VMEM((width,), bf16),
+            pltpu.VMEM((width,), bf16),
+            pltpu.VMEM((rows, width), bf16),
+            pltpu.VMEM((rows, dim), bf16),
+            pltpu.VMEM((rows, dim), bf16),
             pltpu.VMEM((n_tile, width, tile), bf16),
             pltpu.VMEM((n_tile, width, tile), bf16),
             pltpu.VMEM((n_tile, units, tile), bf16),
@@ -380,7 +418,7 @@
             pltpu.VMEM((4, n_tile, rows, tile), f32),
             pltpu.VMEM((4, n_tile, rows, tile), f32),
             pltpu.VMEM((2, 3, n_tile, rows // 2, tile), f32),
-            sems((3, n_tile)), sems((n_tile,)), sems((2,)), sems((n_tile,)), sems((slots,)), sems((slots,)),
+            sems((5,)), sems((6,)), sems((3, n_tile)), sems((n_tile,)), sems((2,)), sems((n_tile,)), sems((slots,)), sems((slots,)),
             sems((2, 9)), sems((2, 9)),
             sems((4, n_tile)), sems((4, n_tile)),
             sems((2, 3, 2, n_tile)), sems((2, 3, 2, n_tile)),
@@ -389,6 +427,32 @@
         cost_estimate=pl.CostEstimate(flops=48 * rows * width * units, bytes_accessed=4 * rows * ctx * dim + 10 * width * width, transcendentals=0),
         name='layer',
     )(hidden_in, cache_len, freq, norm_attn, norm_mlp, k_cache, v_cache, w_q, w_k, w_v, w_o, w_gate, w_up, w_down)
+    return hand_on(*results)
+
+
+def hand_on_kernel(count, *refs):
+    src, dst, buf, sem = refs[:count], refs[count:2 * count], refs[2 * count:3 * count], refs[3 * count]
+    loads = [pltpu.make_async_copy(src[i], buf[i], sem.at[0, i]) for i in range(count)]
+    stores = [pltpu.make_async_copy(buf[i], dst[i], sem.at[1, i]) for i in range(count)]
+    for copy in loads:
+        copy.start()
+    for load, store in zip(loads, stores):
+        load.wait()
+        store.start()
+    for copy in stores:
+        copy.wait()
+
+
+def hand_on(*arrays):
+    hbm = pl.BlockSpec(memory_space=pl.ANY)
+    return pl.pallas_call(
+        functools.partial(hand_on_kernel, len(arrays)),
+        out_shape=[jax.ShapeDtypeStruct(a.shape, a.dtype) for a in arrays],
+        in_specs=[hbm] * len(arrays),
+        out_specs=[hbm] * len(arrays),
+        scratch_shapes=[pltpu.VMEM(a.shape, a.dtype) for a in arrays] + [pltpu.SemaphoreType.DMA((2, len(arrays)))],
+        name='hand_on',
+    )(*arrays)
 
 
 def solution(mesh):

time: 88.6 us -> 82.2 us (0.928)
  local copies, waits for them, and re-layouts: 4.83 us -> 0 us
  Pallas kernels: 82.9 us -> 81.2 us
    unnamed x3 -> x0, local copies, waits for them, and re-layouts: 4.83 us -> none
    pallas_call x1, Pallas kernels: 82.9 us -> 79.3 us  [layer(): pl.pallas_call(functools.partial(layer_kernel, group), out_shape=[jax.Sha...]
    pallas_call x0 -> x1, Pallas kernels: none -> 1.92 us  [hand_on(): pl.pallas_call(functools.partial(hand_on_kernel, len(arrays)), out_shape=...]
where the time goes in v4:
time: 82.2 us; the launch traced here: 82.1 us
  Pallas kernels  81.2 us (99%)
    pallas_call x1, Pallas kernels, layer(): pl.pallas_call(functools.partial(layer_kernel, group), out_shape=[jax.Sha...  79.3 us
    pallas_call x1, Pallas kernels, hand_on(): pl.pallas_call(functools.partial(hand_on_kernel, len(arrays)), out_shape=...  1.92 us

profile of v4, /device:TPU:81, one launch (start us, length us, event | category | flops | bytes accessed | tf_op | source)
XLA Modules:
  0.0 82.1 jit_solution(13222561487858943095)
XLA Ops:
  0.6 79.3 %layer.1 = (bf16[128,2048]{1,0:T(8,128)(2,1)}, bf16[128,256]{1,0:T(8,128)(2,1)}, bf16[128,256]{1,0:T(8,128)(2,1)}) custom-call(bf16[128,2048]{1,0:T(8,128)(2,1)} %x_hbm.1, s32[128]{0:T(128)} %len_hbm.1, f32[1,128]{1,0:T(1,128)} %constant.2.clone.freq_hbm, bf16[2048]{0:T(1024)(128)(2,1)} %gain_hbm.1, bf16[2048]{0:T(1024)(128)(2,1)} %gain2_hbm.1, ...), custom_call_target="tpu_custom_call" | custom-call | flops 25769803776 | bytes 75497472 | tf_op jit(solution)/shard_map/layer/pallas_call | solution.py:387
  80.0 1.9 %hand_on.1 = (bf16[128,2048]{1,0:T(8,128)(2,1)}, bf16[128,256]{1,0:T(8,128)(2,1)}, bf16[128,256]{1,0:T(8,128)(2,1)}) custom-call(bf16[128,2048]{1,0:T(8,128)(2,1)} %get-tuple-element.6.refs_0_, bf16[128,256]{1,0:T(8,128)(2,1)} %get-tuple-element.7.refs_1_, bf16[128,256]{1,0:T(8,128)(2,1)} %get-tuple-element.8.refs_2_), custom_call_target="tpu_custom_call" | custom-call | tf_op jit(solution)/shard_map/hand_on/pallas_call | solution.py:448

commit v5 on v4

--- a/solution.py
+++ b/solution.py
@@ -13,7 +13,7 @@
 
 def layer_kernel(group, x_hbm, len_hbm, freq_hbm, gain_hbm, gain2_hbm, k_hbm, v_hbm, wq_hbm, wk_hbm, wv_hbm, wo_hbm,
                  wg_hbm, wu_hbm, wd_hbm, out_hbm, k_out, v_out,
-                 x_ref, len_ref, freq_ref, gain_ref, gain2_ref, out_ref, k_ref, v_ref, wg, wu, wd, wkv, kbuf, vbuf, xs, qbuf, obuf, sbuf, knew, vnew, turn, x1, xb, hid, own, snd, prt, ring,
+                 x_ref, len_ref, freq_ref, gain_ref, gain2_ref, out_ref, k_ref, v_ref, wg, wu, wd, kbuf, vbuf, xs, qbuf, obuf, sbuf, knew, vnew, turn, x1, xb, hid, own, snd, prt, ring,
                  x_sem, y_sem, w_sem, q_sem, kv_sem, o_sem, k_sem, v_sem, ag_send, ag_recv, d_send, d_recv, r_send, r_recv):
     chips = lax.axis_size('tp') // 2
     me = lax.axis_index('tp')
@@ -59,7 +59,7 @@
         return fetch(wd_hbm, wd, n, w_sem.at[2, n])
 
     def kv_load(i):
-        return pltpu.make_async_copy((wk_hbm, wv_hbm)[i], wkv.at[i], kv_sem.at[i])
+        return pltpu.make_async_copy((wk_hbm, wv_hbm)[i], wg.at[0, :, pl.ds(i * dim, dim)], kv_sem.at[i])
 
     def first_row(g):
         j = lax.rem(g, per_part)
@@ -103,7 +103,7 @@
         return a * cos_t - b * sin_t, b * cos_t + a * sin_t
 
     kv_load(0).wait()
-    kk = jnp.dot(xs[...], wkv[0], preferred_element_type=jnp.float32)
+    kk = jnp.dot(xs[...], wg[0, :, 0:dim], preferred_element_type=jnp.float32)
     ka, kb = rotate(kk[:, :half], kk[:, half:])
     ka, kb = ka.astype(jnp.bfloat16), kb.astype(jnp.bfloat16)
     k_ref[:, :half] = ka
@@ -111,7 +111,7 @@
     knew[:, :half] = ka.astype(jnp.float32)
     knew[:, half:] = kb.astype(jnp.float32)
     kv_load(1).wait()
-    vv = jnp.dot(xs[...], wkv[1], preferred_element_type=jnp.float32).astype(jnp.bfloat16)
+    vv = jnp.dot(xs[...], wg[0, :, dim:2 * dim], preferred_element_type=jnp.float32).astype(jnp.bfloat16)
     v_ref[...] = vv
     vnew[...] = vv.astype(jnp.float32)
     outs = [pltpu.make_async_copy(k_ref, k_out, y_sem.at[0]), pltpu.make_async_copy(v_ref, v_out, y_sem.at[1])]
@@ -181,6 +181,12 @@
             gate_load(g - (groups - n_tile)).start()
         return carry
 
+    def place(s, kind):
+        return {'direct': ((0, 0), (2, 2)), 'end': ((0, 2), (3, 0)), 'far': ((1, 0), (2, 0)), 'own': ((1, 2), (3, 2))}[kind][s]
+
+    def own_at(s):
+        return place(s, 'own')
+
     def finish(s):
         for h in range(heads):
             spot = pl.ds(h, side, stride=heads)
@@ -198,7 +204,7 @@
             if s == 1:
                 up_load(n).start()
             return carry
-        lax.fori_loop(0, n_tile, project, 0)
+        lax.fori_loop(0, n_tile, project, 0, unroll=True)
         if s == 1:
             arrive(0, 1, 3)
             gather(0, 7).start()
@@ -206,28 +212,37 @@
             mid = x1[part, :]
             inv = lax.rsqrt(jnp.mean(mid * mid, axis=-1, keepdims=True) + 1e-6)
             normed = (mid * inv * (1.0 + gain2_ref[...].astype(jnp.float32)[None])).astype(jnp.bfloat16)
-            xb[2 * s + 1, side + j * quart:side + (j + 1) * quart, :] = normed
+            spot = own_at(s)[1] + j
+            xb[own_at(s)[0], spot * quart:(spot + 1) * quart, :] = normed
 
     def span(i, n=1):
         return pl.ds(i * quart, n * quart)
 
     def gather(s, i):
-        near, far = 2 * s, 2 * s + 1
+        def at(kind, k, n=1):
+            b, first = place(s, kind)
+            return xb.at[b, span(first + k, n)]
+
+        def both(kind):
+            b, first = place(s, kind)
+            return at(kind, 0, 2), xb.at[b, span(first + 4, 2)], partner
+
         src, dst, dev = (
-            (xb.at[far, span(2)], xb.at[near, span(1)], ahead),
-            (xb.at[far, span(3)], xb.at[near, span(3)], ahead),
-            (xb.at[far, span(3)], xb.at[near, span(0)], behind),
-            (xb.at[far, span(2)], xb.at[near, span(2)], behind),
-            (xb.at[near, span(1)], xb.at[far, span(0)], ahead),
-            (xb.at[near, span(0)], xb.at[far, span(1)], behind),
-            (xb.at[near, span(0, 2)], xb.at[near, span(4, 2)], partner),
-            (xb.at[near, span(2, 2)], xb.at[near, span(6, 2)], partner),
-            (xb.at[far, span(0, 4)], xb.at[far, span(4, 4)], partner),
+            (at('own', 0), at('direct', 1), ahead),
+            (at('own', 1), at('end', 1), ahead),
+            (at('own', 1), at('direct', 0), behind),
+            (at('own', 0), at('end', 0), behind),
+            (at('direct', 1), at('far', 0), ahead),
+            (at('direct', 0), at('far', 1), behind),
+            both('direct'),
+            both('end'),
+            both('far'),
+            both('own'),
         )[i]
         return to(src, dst, ag_send.at[s, i], ag_recv.at[s, i], dev)
 
     def send(s):
-        for i in (0, 2, 1, 3):
+        for i in (0, 2, 1, 3, 9):
             gather(s, i).start()
 
     def arrive(s, *ids):
@@ -265,22 +280,25 @@
         return to(snd.at[b, n], prt.at[b, n], d_send.at[b, n], d_recv.at[b, n], partner)
 
     def hops(s, step, n):
-        b = (2 * s, 2 * s + 1, 2 * s)[step]
-        fwd = (0, 0, 2)[step]
+        b, fwd = place(s, ('direct', 'far', 'end')[step])
         return (to(own.at[b, n, span(fwd)], ring.at[s, step, n, span(0)], r_send.at[s, step, 0, n], r_recv.at[s, step, 0, n], ahead),
                 to(own.at[b, n, span(fwd + 1)], ring.at[s, step, n, span(1)], r_send.at[s, step, 1, n], r_recv.at[s, step, 1, n], behind))
 
     def merge(b, n):
         swap(b, n).wait_recv()
         own[b, n] = own[b, n] + prt[b, n]
-        for copy in hops(b // 2, b % 2, n):
-            copy.start()
+        for s, step in (((0, 0),), ((0, 1),), ((1, 1), (1, 0)), ())[b]:
+            for copy in hops(s, step, n):
+                copy.start()
 
     pending = []
 
-    def flush(keep=0):
+    def flush(keep=0, after=None):
         while len(pending) > keep:
-            merge(*pending.pop(0))
+            b, n = pending.pop(0)
+            merge(b, n)
+            if after is not None:
+                after(n)
 
     def up(b, after=None):
         for n in range(n_tile):
@@ -289,7 +307,7 @@
             if after is not None:
                 after(n)
 
-    def down(b):
+    def down(b, after=None):
         for n in range(n_tile):
             if b == 0:
                 down_load(n).wait()
@@ -298,12 +316,13 @@
             snd[b, n] = part[rows:2 * rows]
             swap(b, n).start()
             pending.append((b, n))
-            flush(2)
+            flush(2, after)
 
     def relay(s, n):
         for copy in hops(s, 1, n):
             copy.wait_recv()
-        own[2 * s, n, span(2, 2)] = own[2 * s, n, span(2, 2)] + ring[s, 1, n]
+        b, first = place(s, 'end')
+        own[b, n, span(first, 2)] = own[b, n, span(first, 2)] + ring[s, 1, n]
         for copy in hops(s, 2, n):
             copy.start()
 
@@ -313,9 +332,9 @@
                 copy.wait_recv()
         cols = slice(n * tile, (n + 1) * tile)
         a, b = pl.ds(s * quart, quart), pl.ds(side + s * quart, quart)
-        far = 2 * s + 1
-        out_ref[a, cols] = (x1[a, cols] + (own[far, n, span(2)] + (ring[s, 0, n, span(1)] + ring[s, 2, n, span(0)]))).astype(jnp.bfloat16)
-        out_ref[b, cols] = (x1[b, cols] + (own[far, n, span(3)] + (ring[s, 0, n, span(0)] + ring[s, 2, n, span(1)]))).astype(jnp.bfloat16)
+        mine, first = place(s, 'own')
+        out_ref[a, cols] = (x1[a, cols] + (own[mine, n, span(first)] + (ring[s, 0, n, span(1)] + ring[s, 2, n, span(0)]))).astype(jnp.bfloat16)
+        out_ref[b, cols] = (x1[b, cols] + (own[mine, n, span(first + 1)] + (ring[s, 0, n, span(0)] + ring[s, 2, n, span(1)]))).astype(jnp.bfloat16)
 
     def give(s):
         a, b = pl.ds(s * quart, quart), pl.ds(side + s * quart, quart)
@@ -332,31 +351,27 @@
     down(0)
     arrive(1, 1, 3)
     gather(1, 7).start()
-    arrive(0, 8)
+    arrive(0, 8, 9)
     up(1)
-    down(1)
     arrive(1, 4, 5)
     gather(1, 8).start()
-    arrive(1, 6, 7)
+    down(1)
+    arrive(1, 6, 8)
     up(2, lambda n: relay(0, n))
     down(2)
-    arrive(1, 8)
+    arrive(1, 7, 9)
     up(3)
-    down(3)
-    settle(0, 0)
-    settle(0, 1)
-    flush()
-    for n in range(2, n_tile):
+    down(3, lambda n: relay(1, n))
+    for n in range(n_tile):
         settle(0, n)
     give(0)
-    for n in range(n_tile):
-        relay(1, n)
+    flush(0, lambda n: relay(1, n))
     for n in range(n_tile):
         settle(1, n)
     give(1)
 
     for s in range(2):
-        for i in range(9):
+        for i in range(10):
             gather(s, i).wait_send()
 
     def drain(n, carry):
@@ -401,7 +416,6 @@
             pltpu.VMEM((n_tile, width, tile), bf16),
             pltpu.VMEM((n_tile, width, tile), bf16),
             pltpu.VMEM((n_tile, units, tile), bf16),
-            pltpu.VMEM((2, width, dim), bf16),
             pltpu.VMEM((slots, group, ctx, dim), bf16),
             pltpu.VMEM((slots, group, ctx, dim), bf16),
             pltpu.VMEM((rows, width), bf16),
@@ -419,7 +433,7 @@
             pltpu.VMEM((4, n_tile, rows, tile), f32),
             pltpu.VMEM((2, 3, n_tile, rows // 2, tile), f32),
             sems((5,)), sems((6,)), sems((3, n_tile)), sems((n_tile,)), sems((2,)), sems((n_tile,)), sems((slots,)), sems((slots,)),
-            sems((2, 9)), sems((2, 9)),
+            sems((2, 10)), sems((2, 10)),
             sems((4, n_tile)), sems((4, n_tile)),
             sems((2, 3, 2, n_tile)), sems((2, 3, 2, n_tile)),
         ],

time: 82.2 us -> 79.9 us (0.972)
  Pallas kernels: 81.2 us -> 79 us
    pallas_call x1, Pallas kernels: 79.3 us -> 77.1 us  [layer(): pl.pallas_call(functools.partial(layer_kernel, group), out_shape=[jax.Sha...]
where the time goes in v5:
time: 79.9 us; the launch traced here: 79.8 us
  Pallas kernels  79 us (99%)
  between operations  0.82 us (1%)
    pallas_call x1, Pallas kernels, layer(): pl.pallas_call(functools.partial(layer_kernel, group), out_shape=[jax.Sha...  77.1 us
    pallas_call x1, Pallas kernels, hand_on(): pl.pallas_call(functools.partial(hand_on_kernel, len(arrays)), out_shape=...  1.92 us

profile of v5, /device:TPU:81, one launch (start us, length us, event | category | flops | bytes accessed | tf_op | source)
XLA Modules:
  0.0 79.8 jit_solution(9973873453437321247)
XLA Ops:
  0.6 77.1 %layer.1 = (bf16[128,2048]{1,0:T(8,128)(2,1)}, bf16[128,256]{1,0:T(8,128)(2,1)}, bf16[128,256]{1,0:T(8,128)(2,1)}) custom-call(bf16[128,2048]{1,0:T(8,128)(2,1)} %x_hbm.1, s32[128]{0:T(128)} %len_hbm.1, f32[1,128]{1,0:T(1,128)} %constant.2.clone.freq_hbm, bf16[2048]{0:T(1024)(128)(2,1)} %gain_hbm.1, bf16[2048]{0:T(1024)(128)(2,1)} %gain2_hbm.1, ...), custom_call_target="tpu_custom_call" | custom-call | flops 25769803776 | bytes 75497472 | tf_op jit(solution)/shard_map/layer/pallas_call | solution.py:402
  77.7 1.9 %hand_on.1 = (bf16[128,2048]{1,0:T(8,128)(2,1)}, bf16[128,256]{1,0:T(8,128)(2,1)}, bf16[128,256]{1,0:T(8,128)(2,1)}) custom-call(bf16[128,2048]{1,0:T(8,128)(2,1)} %get-tuple-element.6.refs_0_, bf16[128,256]{1,0:T(8,128)(2,1)} %get-tuple-element.7.refs_1_, bf16[128,256]{1,0:T(8,128)(2,1)} %get-tuple-element.8.refs_2_), custom_call_target="tpu_custom_call" | custom-call | tf_op jit(solution)/shard_map/hand_on/pallas_call | solution.py:462
